TPU v7x, 256 devices: a whole 4x4x8 slice. The times are simulated.
256 devices in a mesh: gy: 16 (over y, x_hi, core), gx: 16 (over z, x_lo).
Axes of the slice: x: 4 (x_hi: 2, x_lo: 2; x = x_hi * 2 + x_lo), y: 4, z: 8, core: 2. Of those that a mesh axis runs over, the one named last changes fastest.
Arguments:
- ice_velocity: float32 [2, 3584, 2048], P(None, 'gy', 'gx'), may hold values from -6 to 6
- ice_stress: float32 [3, 3584, 2048], P(None, 'gy', 'gx'), may hold values from -3 to 3
- ice_mass: float32 [3584, 2048], P('gy', 'gx'), may hold values from 0.5 to 4
- ice_strength: float32 [3584, 2048], P('gy', 'gx'), may hold values from 0.5 to 4
- wind_stress: float32 [2, 3584, 2048], P(None, 'gy', 'gx'), may hold values from -3 to 3
- sea_level: float32 [3584, 2048], P('gy', 'gx'), may hold values from -3 to 3
- transport: float32 [2, 3584, 2048], P(None, 'gy', 'gx'), may hold values from -6 to 6
- depth: float32 [3584, 2048], P('gy', 'gx'), may hold values from 0.5 to 2
- land_mask: int32 [3584, 2048], P('gy', 'gx'), may hold values 0 or 1
- ice_mask: int32 [3584, 2048], P('gy', 'gx'), may hold values 0 or 1
- fold_partner: int32 [2048], P('gx'), may hold values from 0 to 2047, as said below
Outputs:
- ice_velocity_out: float32 [2, 3584, 2048], P(None, 'gy', 'gx')
- ice_stress_out: float32 [3, 3584, 2048], P(None, 'gy', 'gx')
- sea_level_out: float32 [3584, 2048], P('gy', 'gx')
- transport_out: float32 [2, 3584, 2048], P(None, 'gy', 'gx')
Inputs may be any that keep to these rules, and one draw needn't show every extreme that they name: fold_partner names each column once, and the partner of column i lies among the columns 128 * (15 - i // 128) to 128 * (16 - i // 128) - 1.
All inputs are finite; a program needn't handle non-finite values. No bound on the sum of `land_mask` or of `ice_mask` on one device may be relied on, other than what follows from the above.
Results may differ from a plain program's by a relative error of at most 0.00014.
Values sent between devices are 32-bit elements; how exact they have to be, the bound alone decides.
A program may use at most 64 MiB of HBM per device.

v0:
```python
import jax
import jax.numpy as jnp
from jax import lax
from jax.sharding import PartitionSpec as P

EVP_ITERS = 4
SUBSTEPS = 6


DT_ICE = 1.0
DT_SEA = 0.5
CDW = 0.5
ALPHA_MIN = 2.0
ALPHA_C = 16.0
INV_E2 = 0.25
DMIN = 0.05
FCOR = 0.5
GRAV = 1.0
RBOT = 0.2


def from_partner(value, axis, bit):
    mask = 2**bit
    pairs = [(source, source ^ mask) for source in range(lax.axis_size(axis))]
    return lax.ppermute(value, axis, pairs)


def extended_2(cells, sides, width, closed):
    for axis, dim in sides:
        count = lax.axis_size(axis)
        ends = count if closed else count - 1
        head = lax.slice_in_dim(cells, 0, width, axis=dim)
        tail = lax.slice_in_dim(cells, cells.shape[dim] - width, cells.shape[dim], axis=dim)
        cells = jnp.concatenate(
            [
                lax.ppermute(tail, axis, [(i, (i + 1) % count) for i in range(ends)]),
                cells,
                lax.ppermute(head, axis, [((i + 1) % count, i) for i in range(ends)]),
            ],
            axis=dim,
        )
    return cells


def centre_x(field):
    return (field[..., 1:-1, 2:] - field[..., 1:-1, :-2]) * 0.5


def centre_y(field):
    return (field[..., 2:, 1:-1] - field[..., :-2, 1:-1]) * 0.5


def interior(field):
    return field[..., 1:-1, 1:-1]


def latitude_factor(row_index, total_rows):
    angle_rows = jnp.pi * ((row_index.astype(jnp.float32) + 0.5) / total_rows - 0.5)
    return (FCOR * jnp.sin(angle_rows))[:, None]


def rheology(extended, statics, start_velocity, ocean_velocity, wind_stress, coriolis):
    ice_u = extended[0, 2:-2, 2:-2]
    ice_v = extended[1, 2:-2, 2:-2]
    strain_xx = centre_x(extended[0])
    strain_yy = centre_y(extended[1])
    shear_rate = centre_y(extended[0]) + centre_x(extended[1])
    divergence = strain_xx + strain_yy
    tension = strain_xx - strain_yy
    deformation = jnp.sqrt(
        divergence * divergence
        + (tension * tension + shear_rate * shear_rate) * INV_E2
        + DMIN * DMIN
    )
    strength = interior(statics[0])
    ice_cover = interior(statics[2] * statics[3])
    mass_rim = interior(statics[1]) + 1.0 - ice_cover
    relaxation = ALPHA_MIN + jnp.sqrt(ALPHA_C * strength / mass_rim)
    stress_sum = (
        ice_cover
        * (relaxation * interior(extended[2]) + strength * (divergence / deformation - 1.0))
        / (1.0 + relaxation)
    )
    stress_diff = (
        ice_cover
        * (relaxation * interior(extended[3]) + strength * tension * INV_E2 / deformation)
        / (1.0 + relaxation)
    )
    stress_xy = (
        ice_cover
        * (
            relaxation * interior(extended[4])
            + strength * shear_rate * (0.5 * INV_E2) / deformation
        )
        / (1.0 + relaxation)
    )
    stress_xx = 0.5 * (stress_sum + stress_diff)
    stress_yy = 0.5 * (stress_sum - stress_diff)
    force_x = centre_x(stress_xx) + centre_y(stress_xy)
    force_y = centre_x(stress_xy) + centre_y(stress_yy)
    inertia = interior(relaxation)
    mass_cell = interior(mass_rim)
    cover_cell = interior(ice_cover)
    rel_x = ocean_velocity[0] - ice_u
    rel_y = ocean_velocity[1] - ice_v
    drag_coef = CDW * jnp.sqrt(rel_x * rel_x + rel_y * rel_y)
    denominator = 1.0 + inertia + DT_ICE * drag_coef / mass_cell
    new_u = (
        cover_cell
        * (
            inertia * ice_u
            + start_velocity[0]
            + DT_ICE / mass_cell * (force_x + wind_stress[0] + drag_coef * ocean_velocity[0])
            + DT_ICE * coriolis * ice_v
        )
        / denominator
    )
    new_v = (
        cover_cell
        * (
            inertia * ice_v
            + start_velocity[1]
            + DT_ICE / mass_cell * (force_y + wind_stress[1] + drag_coef * ocean_velocity[1])
            - DT_ICE * coriolis * ice_u
        )
        / denominator
    )
    return jnp.stack(
        [new_u, new_v, interior(stress_sum), interior(stress_diff), interior(stress_xy)]
    )


def barotropic(extended, land_rim, depth, surface_stress, coriolis):
    new_level = interior(land_rim) * (
        interior(extended[0]) - DT_SEA * (centre_x(extended[1]) + centre_y(extended[2]))
    )
    flow_x = extended[1, 2:-2, 2:-2]
    flow_y = extended[2, 2:-2, 2:-2]
    land_cell = land_rim[2:-2, 2:-2]
    damping = 1.0 + DT_SEA * RBOT / depth
    next_x = (
        land_cell
        * (
            flow_x
            - DT_SEA * (GRAV * depth * centre_x(new_level) - coriolis * flow_y - surface_stress[0])
        )
        / damping
    )
    next_y = (
        land_cell
        * (
            flow_y
            - DT_SEA * (GRAV * depth * centre_y(new_level) + coriolis * flow_x - surface_stress[1])
        )
        / damping
    )
    return jnp.stack([interior(new_level), next_x, next_y])


def make_selector(fold_partner, col_count):
    offset = (lax.axis_size("gx") - 1 - lax.axis_index("gx")) * col_count
    local_index = fold_partner - offset
    sources = jnp.arange(col_count, dtype=jnp.int32)
    return (sources[:, None] == local_index[None, :]).astype(jnp.float32)


def extend(field_stack, sign_list, selector):
    flipped = jnp.flip(field_stack[:, -2:, :], axis=1)
    bit_total = lax.axis_size("gx").bit_length() - 1
    bit_order = list(range(bit_total))
    mirrored = flipped
    for bit_number in bit_order:
        mirrored = from_partner(mirrored, "gx", bit_number)
    fold_part = jnp.einsum("fkc,cd->fkd", mirrored, selector, precision=lax.Precision.HIGHEST)
    fold_part = fold_part * sign_list[:, None, None]
    row_extended = extended_2(field_stack, (("gy", 1),), 2, False)
    is_top = lax.axis_index("gy") == lax.axis_size("gy") - 1
    north_part = jnp.where(is_top, fold_part, row_extended[:, -2:, :])
    row_extended = jnp.concatenate([row_extended[:, :-2, :], north_part], axis=1)
    return extended_2(row_extended, (("gx", 2),), 2, True)


def per_device(
    ice_velocity,
    ice_stress,
    ice_mass,
    ice_strength,
    wind_stress,
    sea_level,
    transport,
    depth,
    land_mask,
    ice_mask,
    fold_partner,
):
    row_count = sea_level.shape[0]
    total_rows = row_count * lax.axis_size("gy")
    row_index = lax.axis_index("gy") * row_count + jnp.arange(row_count, dtype=jnp.int32)
    coriolis = latitude_factor(row_index, total_rows)
    selector = make_selector(fold_partner, sea_level.shape[1])
    ocean_velocity = transport / depth[None]
    static_signs = jnp.array([1.0, 1.0, 1.0, 1.0], jnp.float32)
    ice_signs = jnp.array([-1.0, -1.0, 1.0, 1.0, 1.0], jnp.float32)
    sea_signs = jnp.array([1.0, -1.0, -1.0], jnp.float32)
    statics = extend(
        jnp.stack(
            [ice_strength, ice_mass, land_mask.astype(jnp.float32), ice_mask.astype(jnp.float32)]
        ),
        static_signs,
        selector,
    )
    ice_state = jnp.concatenate([ice_velocity, ice_stress], axis=0)
    for iteration in range(EVP_ITERS):
        ice_state = rheology(
            extend(ice_state, ice_signs, selector),
            statics,
            ice_velocity,
            ocean_velocity,
            wind_stress,
            coriolis,
        )
    final_velocity = ice_state[:2]
    cover_cell = statics[2, 2:-2, 2:-2] * statics[3, 2:-2, 2:-2]
    rel_x = final_velocity[0] - ocean_velocity[0]
    rel_y = final_velocity[1] - ocean_velocity[1]
    drag_coef = CDW * jnp.sqrt(rel_x * rel_x + rel_y * rel_y)
    surface_stress = (
        cover_cell * drag_coef * (final_velocity - ocean_velocity)
        + (1.0 - cover_cell) * wind_stress
    )
    sea_state = jnp.concatenate([sea_level[None], transport], axis=0)
    for substep in range(SUBSTEPS):
        sea_state = barotropic(
            extend(sea_state, sea_signs, selector), statics[2], depth, surface_stress, coriolis
        )
    return (final_velocity, ice_state[2:], sea_state[0], sea_state[1:])


def solution(mesh):
    in_specs = (
        P(None, "gy", "gx"),
        P(None, "gy", "gx"),
        P("gy", "gx"),
        P("gy", "gx"),
        P(None, "gy", "gx"),
        P("gy", "gx"),
        P(None, "gy", "gx"),
        P("gy", "gx"),
        P("gy", "gx"),
        P("gy", "gx"),
        P("gx"),
    )
    out_specs = (P(None, "gy", "gx"), P(None, "gy", "gx"), P("gy", "gx"), P(None, "gy", "gx"))
    return jax.shard_map(
        per_device, mesh=mesh, in_specs=in_specs, out_specs=out_specs, check_vma=False
    )
```

profile of v0, /device:TPU:8, one launch (start us, length us, event | category | flops | bytes accessed | tf_op | source)
XLA Modules:
  0.0 583.4 jit_solution(5779003680208189470)
XLA Ops:
  22.5 6.9 %collective-permute-done.9 = f32[5,2,128]{1,2,0:T(8,128)} collective-permute-done((f32[5,2,128]{1,2,0:T(8,128)}, f32[5,2,128]{1,2,0:T(8,128)}, u32[]{:S(2)}, u32[]{:S(2)}) %collective-permute-start.9) | collective-permute-done | bytes 5152 | tf_op jit(solution)/shard_map/ppermute | solution.py:25
  34.6 8.8 %collective-permute-done.10 = f32[5,2,128]{1,2,0:T(8,128)} collective-permute-done((f32[5,2,128]{1,2,0:T(8,128)}, f32[5,2,128]{1,2,0:T(8,128)}, u32[]{:S(2)}, u32[]{:S(2)}) %collective-permute-start.10) | collective-permute-done | bytes 5152 | tf_op jit(solution)/shard_map/ppermute | solution.py:25
  51.5 6.4 %collective-permute-start.13 = (f32[5,2,128]{1,2,0:T(8,128)}, f32[5,2,128]{1,2,0:T(8,128)}, u32[]{:S(2)}, u32[]{:S(2)}) collective-permute-start(f32[5,2,128]{1,2,0:T(8,128)} %get-tuple-element.110), channel_id=1, source_target_pairs={{16,0},{32,16},{48,32},{64,48},{80,64},{96,80},{112,96},{128,112},... | collective-permute-start | bytes 15368 | tf_op jit(solution)/shard_map/ppermute | solution.py:38
  57.9 16.1 %collective-permute-done.11 = f32[5,2,128]{1,2,0:T(8,128)} collective-permute-done((f32[5,2,128]{1,2,0:T(8,128)}, f32[5,2,128]{1,2,0:T(8,128)}, u32[]{:S(2)}, u32[]{:S(2)}) %collective-permute-start.11) | collective-permute-done | bytes 5152 | tf_op jit(solution)/shard_map/ppermute | solution.py:25
  74.0 6.3 %collective-permute-start.12 = (f32[5,2,128]{1,2,0:T(8,128)}, f32[5,2,128]{1,2,0:T(8,128)}, u32[]{:S(2)}, u32[]{:S(2)}) collective-permute-start(f32[5,2,128]{1,2,0:T(8,128)} %collective-permute-done.11), channel_id=1, source_target_pairs={{0,8},{1,9},{2,10},{3,11},{4,12},{5,13},{6,14},{7,15},{8,0},{9,1},... | collective-permute-start | bytes 15368 | tf_op jit(solution)/shard_map/ppermute | solution.py:25
  84.4 10.0 %collective-permute-done.12 = f32[5,2,128]{1,2,0:T(8,128)} collective-permute-done((f32[5,2,128]{1,2,0:T(8,128)}, f32[5,2,128]{1,2,0:T(8,128)}, u32[]{:S(2)}, u32[]{:S(2)}) %collective-permute-start.12) | collective-permute-done | bytes 5152 | tf_op jit(solution)/shard_map/ppermute | solution.py:25
  99.2 4.8 collective-permute-start.15
  105.4 4.6 collective-permute-done.14
  116.6 8.4 %collective-permute-done.17 = f32[5,2,128]{1,2,0:T(8,128)S(1)} collective-permute-done((f32[5,2,128]{1,2,0:T(8,128)}, f32[5,2,128]{1,2,0:T(8,128)S(1)}, u32[]{:S(2)}, u32[]{:S(2)}) %collective-permute-start.17) | collective-permute-done | bytes 5152 | tf_op jit(solution)/shard_map/ppermute | solution.py:25
  125.0 7.4 %collective-permute-done.18 = f32[5,2,128]{1,2,0:T(8,128)S(1)} collective-permute-done((f32[5,2,128]{1,2,0:T(8,128)S(1)}, f32[5,2,128]{1,2,0:T(8,128)S(1)}, u32[]{:S(2)}, u32[]{:S(2)}) %collective-permute-start.18) | collective-permute-done | bytes 5152 | tf_op jit(solution)/shard_map/ppermute | solution.py:25
  132.4 14.4 %collective-permute-done.19 = f32[5,2,128]{1,2,0:T(8,128)S(1)} collective-permute-done((f32[5,2,128]{1,2,0:T(8,128)S(1)}, f32[5,2,128]{1,2,0:T(8,128)S(1)}, u32[]{:S(2)}, u32[]{:S(2)}) %collective-permute-start.19) | collective-permute-done | bytes 5152 | tf_op jit(solution)/shard_map/ppermute | solution.py:25
  150.4 6.0 %collective-permute-start.21 = (f32[5,2,128]{1,2,0:T(8,128)}, f32[5,2,128]{1,2,0:T(8,128)}, u32[]{:S(2)}, u32[]{:S(2)}) collective-permute-start(f32[5,2,128]{1,2,0:T(8,128)} %get-tuple-element.108), channel_id=1, source_target_pairs={{16,0},{32,16},{48,32},{64,48},{80,64},{96,80},{112,96},{128,112},... | collective-permute-start | bytes 15368 | tf_op jit(solution)/shard_map/ppermute | solution.py:38
  156.5 8.1 %collective-permute-done.20 = f32[5,2,128]{1,2,0:T(8,128)} collective-permute-done((f32[5,2,128]{1,2,0:T(8,128)S(1)}, f32[5,2,128]{1,2,0:T(8,128)}, u32[]{:S(2)}, u32[]{:S(2)}) %collective-permute-start.20) | collective-permute-done | bytes 5152 | tf_op jit(solution)/shard_map/ppermute | solution.py:25
  183.7 7.9 %collective-permute-done.25 = f32[5,2,128]{1,2,0:T(8,128)} collective-permute-done((f32[5,2,128]{1,2,0:T(8,128)}, f32[5,2,128]{1,2,0:T(8,128)}, u32[]{:S(2)}, u32[]{:S(2)}) %collective-permute-start.25) | collective-permute-done | bytes 5152 | tf_op jit(solution)/shard_map/ppermute | solution.py:25
  193.2 6.7 %collective-permute-done.26 = f32[5,2,128]{1,2,0:T(8,128)} collective-permute-done((f32[5,2,128]{1,2,0:T(8,128)}, f32[5,2,128]{1,2,0:T(8,128)}, u32[]{:S(2)}, u32[]{:S(2)}) %collective-permute-start.26) | collective-permute-done | bytes 5152 | tf_op jit(solution)/shard_map/ppermute | solution.py:25
  203.2 5.9 %collective-permute-done.41 = f32[3,2,128]{1,2,0:T(8,128)S(1)} collective-permute-done((f32[3,2,128]{1,2,0:T(8,128)}, f32[3,2,128]{1,2,0:T(8,128)S(1)}, u32[]{:S(2)}, u32[]{:S(2)}) %collective-permute-start.41) | collective-permute-done | bytes 3104 | tf_op jit(solution)/shard_map/ppermute | solution.py:25
  218.6 5.4 collective-permute-start.43
  226.0 6.0 %collective-permute-start.45 = (f32[3,2,128]{1,2,0:T(8,128)}, f32[3,2,128]{1,2,0:T(8,128)}, u32[]{:S(2)}, u32[]{:S(2)}) collective-permute-start(f32[3,2,128]{1,2,0:T(8,128)} %get-tuple-element.145), channel_id=1, source_target_pairs={{16,0},{32,16},{48,32},{64,48},{80,64},{96,80},{112,96},{128,112},... | collective-permute-start | bytes 9224 | tf_op jit(solution)/shard_map/ppermute | solution.py:38
  232.0 6.0 %collective-permute-done.43 = f32[3,2,128]{1,2,0:T(8,128)} collective-permute-done((f32[3,2,128]{1,2,0:T(8,128)S(1)}, f32[3,2,128]{1,2,0:T(8,128)}, u32[]{:S(2)}, u32[]{:S(2)}) %collective-permute-start.43) | collective-permute-done | bytes 3104 | tf_op jit(solution)/shard_map/ppermute | solution.py:25
  243.4 6.0 %collective-permute-start.29 = (f32[5,2,128]{1,2,0:T(8,128)}, f32[5,2,128]{1,2,0:T(8,128)}, u32[]{:S(2)}, u32[]{:S(2)}) collective-permute-start(f32[5,2,128]{1,2,0:T(8,128)} %get-tuple-element.106), channel_id=1, source_target_pairs={{16,0},{32,16},{48,32},{64,48},{80,64},{96,80},{112,96},{128,112},... | collective-permute-start | bytes 15368 | tf_op jit(solution)/shard_map/ppermute | solution.py:38
  276.1 7.1 %collective-permute-done.33 = f32[5,2,128]{1,2,0:T(8,128)S(1)} collective-permute-done((f32[5,2,128]{1,2,0:T(8,128)}, f32[5,2,128]{1,2,0:T(8,128)S(1)}, u32[]{:S(2)}, u32[]{:S(2)}) %collective-permute-start.33) | collective-permute-done | bytes 5152 | tf_op jit(solution)/shard_map/ppermute | solution.py:25
  284.5 7.6 %collective-permute-done.34 = f32[5,2,128]{1,2,0:T(8,128)S(1)} collective-permute-done((f32[5,2,128]{1,2,0:T(8,128)S(1)}, f32[5,2,128]{1,2,0:T(8,128)S(1)}, u32[]{:S(2)}, u32[]{:S(2)}) %collective-permute-start.34) | collective-permute-done | bytes 5152 | tf_op jit(solution)/shard_map/ppermute | solution.py:25
  293.9 14.0 %collective-permute-done.35 = f32[5,2,128]{1,2,0:T(8,128)S(1)} collective-permute-done((f32[5,2,128]{1,2,0:T(8,128)S(1)}, f32[5,2,128]{1,2,0:T(8,128)S(1)}, u32[]{:S(2)}, u32[]{:S(2)}) %collective-permute-start.35) | collective-permute-done | bytes 5152 | tf_op jit(solution)/shard_map/ppermute | solution.py:25
  307.9 4.7 collective-permute-start.36
  315.3 6.0 %collective-permute-start.37 = (f32[5,2,128]{1,2,0:T(8,128)}, f32[5,2,128]{1,2,0:T(8,128)}, u32[]{:S(2)}, u32[]{:S(2)}) collective-permute-start(f32[5,2,128]{1,2,0:T(8,128)} %get-tuple-element.104), channel_id=1, source_target_pairs={{16,0},{32,16},{48,32},{64,48},{80,64},{96,80},{112,96},{128,112},... | collective-permute-start | bytes 15368 | tf_op jit(solution)/shard_map/ppermute | solution.py:38
  321.3 6.7 %collective-permute-done.36 = f32[5,2,128]{1,2,0:T(8,128)} collective-permute-done((f32[5,2,128]{1,2,0:T(8,128)S(1)}, f32[5,2,128]{1,2,0:T(8,128)}, u32[]{:S(2)}, u32[]{:S(2)}) %collective-permute-start.36) | collective-permute-done | bytes 5152 | tf_op jit(solution)/shard_map/ppermute | solution.py:25
  344.7 5.7 collective-permute-done.49
  350.4 7.8 %collective-permute-done.50 = f32[3,2,128]{1,2,0:T(8,128)S(1)} collective-permute-done((f32[3,2,128]{1,2,0:T(8,128)S(1)}, f32[3,2,128]{1,2,0:T(8,128)S(1)}, u32[]{:S(2)}, u32[]{:S(2)}) %collective-permute-start.50) | collective-permute-done | bytes 3104 | tf_op jit(solution)/shard_map/ppermute | solution.py:25
  360.1 9.8 %collective-permute-done.51 = f32[3,2,128]{1,2,0:T(8,128)S(1)} collective-permute-done((f32[3,2,128]{1,2,0:T(8,128)S(1)}, f32[3,2,128]{1,2,0:T(8,128)S(1)}, u32[]{:S(2)}, u32[]{:S(2)}) %collective-permute-start.51) | collective-permute-done | bytes 3104 | tf_op jit(solution)/shard_map/ppermute | solution.py:25
  371.8 7.6 %collective-permute-done.52 = f32[3,2,128]{1,2,0:T(8,128)S(1)} collective-permute-done((f32[3,2,128]{1,2,0:T(8,128)S(1)}, f32[3,2,128]{1,2,0:T(8,128)S(1)}, u32[]{:S(2)}, u32[]{:S(2)}) %collective-permute-start.52) | collective-permute-done | bytes 3104 | tf_op jit(solution)/shard_map/ppermute | solution.py:25
  387.2 5.7 collective-permute-done.57
  392.8 7.4 %collective-permute-done.58 = f32[3,2,128]{1,2,0:T(8,128)S(1)} collective-permute-done((f32[3,2,128]{1,2,0:T(8,128)S(1)}, f32[3,2,128]{1,2,0:T(8,128)S(1)}, u32[]{:S(2)}, u32[]{:S(2)}) %collective-permute-start.58) | collective-permute-done | bytes 3104 | tf_op jit(solution)/shard_map/ppermute | solution.py:25
  402.1 5.7 collective-permute-done.59
  407.9 14.2 %collective-permute-start.60 = (f32[3,2,128]{1,2,0:T(8,128)S(1)}, f32[3,2,128]{1,2,0:T(8,128)S(1)}, u32[]{:S(2)}, u32[]{:S(2)}) collective-permute-start(f32[3,2,128]{1,2,0:T(8,128)S(1)} %collective-permute-done.59), channel_id=1, source_target_pairs={{0,8},{1,9},{2,10},{3,11},{4,12},{5,13},{6,14},{7,15},{8,0},{9,1},... | collective-permute-start | bytes 9224 | tf_op jit(solution)/shard_map/ppermute | solution.py:25
  426.0 5.4 collective-permute-done.56
  439.1 5.7 collective-permute-done.65
  444.7 7.2 %collective-permute-done.66 = f32[3,2,128]{1,2,0:T(8,128)S(1)} collective-permute-done((f32[3,2,128]{1,2,0:T(8,128)S(1)}, f32[3,2,128]{1,2,0:T(8,128)S(1)}, u32[]{:S(2)}, u32[]{:S(2)}) %collective-permute-start.66) | collective-permute-done | bytes 3104 | tf_op jit(solution)/shard_map/ppermute | solution.py:25
  453.9 14.3 %collective-permute-done.67 = f32[3,2,128]{1,2,0:T(8,128)S(1)} collective-permute-done((f32[3,2,128]{1,2,0:T(8,128)S(1)}, f32[3,2,128]{1,2,0:T(8,128)S(1)}, u32[]{:S(2)}, u32[]{:S(2)}) %collective-permute-start.67) | collective-permute-done | bytes 3104 | tf_op jit(solution)/shard_map/ppermute | solution.py:25
  470.1 7.6 %collective-permute-done.68 = f32[3,2,128]{1,2,0:T(8,128)S(1)} collective-permute-done((f32[3,2,128]{1,2,0:T(8,128)S(1)}, f32[3,2,128]{1,2,0:T(8,128)S(1)}, u32[]{:S(2)}, u32[]{:S(2)}) %collective-permute-start.68) | collective-permute-done | bytes 3104 | tf_op jit(solution)/shard_map/ppermute | solution.py:25
  485.4 5.7 collective-permute-done.73
  491.0 5.7 collective-permute-done.74
  498.8 6.0 %collective-permute-done.75 = f32[3,2,128]{1,2,0:T(8,128)S(1)} collective-permute-done((f32[3,2,128]{1,2,0:T(8,128)S(1)}, f32[3,2,128]{1,2,0:T(8,128)S(1)}, u32[]{:S(2)}, u32[]{:S(2)}) %collective-permute-start.75) | collective-permute-done | bytes 3104 | tf_op jit(solution)/shard_map/ppermute | solution.py:25
  504.8 14.4 %collective-permute-start.76 = (f32[3,2,128]{1,2,0:T(8,128)S(1)}, f32[3,2,128]{1,2,0:T(8,128)S(1)}, u32[]{:S(2)}, u32[]{:S(2)}) collective-permute-start(f32[3,2,128]{1,2,0:T(8,128)S(1)} %collective-permute-done.75), channel_id=1, source_target_pairs={{0,8},{1,9},{2,10},{3,11},{4,12},{5,13},{6,14},{7,15},{8,0},{9,1},... | collective-permute-start | bytes 9224 | tf_op jit(solution)/shard_map/ppermute | solution.py:25
  523.1 5.4 collective-permute-done.72
  535.9 5.7 collective-permute-done.81
  541.6 6.6 %collective-permute-done.82 = f32[3,2,128]{1,2,0:T(8,128)S(1)} collective-permute-done((f32[3,2,128]{1,2,0:T(8,128)S(1)}, f32[3,2,128]{1,2,0:T(8,128)S(1)}, u32[]{:S(2)}, u32[]{:S(2)}) %collective-permute-start.82) | collective-permute-done | bytes 3104 | tf_op jit(solution)/shard_map/ppermute | solution.py:25
  550.6 14.1 %collective-permute-done.83 = f32[3,2,128]{1,2,0:T(8,128)S(1)} collective-permute-done((f32[3,2,128]{1,2,0:T(8,128)S(1)}, f32[3,2,128]{1,2,0:T(8,128)S(1)}, u32[]{:S(2)}, u32[]{:S(2)}) %collective-permute-start.83) | collective-permute-done | bytes 3104 | tf_op jit(solution)/shard_map/ppermute | solution.py:25
  566.7 7.5 %collective-permute-done.84 = f32[3,2,128]{1,2,0:T(8,128)S(1)} collective-permute-done((f32[3,2,128]{1,2,0:T(8,128)S(1)}, f32[3,2,128]{1,2,0:T(8,128)S(1)}, u32[]{:S(2)}, u32[]{:S(2)}) %collective-permute-start.84) | collective-permute-done | bytes 3104 | tf_op jit(solution)/shard_map/ppermute | solution.py:25
  (318 shorter events, 207.3 us)
Async XLA Ops:
  4.4 47.1 %collective-permute-start.5 = (f32[4,2,128]{1,2,0:T(8,128)}, f32[4,2,128]{1,2,0:T(8,128)}, u32[]{:S(2)}, u32[]{:S(2)}) collective-permute-start(f32[4,2,128]{1,2,0:T(8,128)} %get-tuple-element.115), channel_id=1, source_target_pairs={{16,0},{32,16},{48,32},{64,48},{80,64},{96,80},{112,96},{128,112},... | collective-permute-start | bytes 12296 | tf_op jit(solution)/shard_map/ppermute | solution.py:38
  8.7 73.0 %collective-permute-start = (f32[4,2,128]{1,2,0:T(8,128)S(1)}, f32[4,2,128]{1,2,0:T(8,128)S(1)}, u32[]{:S(2)}, u32[]{:S(2)}) collective-permute-start(f32[4,2,128]{1,2,0:T(8,128)S(1)} %get-tuple-element.114), channel_id=1, source_target_pairs={{0,16},{16,32},{32,48},{48,64},{64,80},{80,96},{96,112},{112,128},... | collective-permute-start | bytes 12296 | tf_op jit(solution)/shard_map/ppermute | solution.py:36
  13.1 85.2 %collective-permute-start.8 = (f32[5,2,128]{1,2,0:T(8,128)S(1)}, f32[5,2,128]{1,2,0:T(8,128)}, u32[]{:S(2)}, u32[]{:S(2)}) collective-permute-start(f32[5,2,128]{1,2,0:T(8,128)S(1)} %get-tuple-element.109), channel_id=1, source_target_pairs={{0,16},{16,32},{32,48},{48,64},{64,80},{80,96},{96,112},{112,128},... | collective-permute-start | bytes 15368 | tf_op jit(solution)/shard_map/ppermute | solution.py:36
  18.5 10.9 %collective-permute-start.9 = (f32[5,2,128]{1,2,0:T(8,128)}, f32[5,2,128]{1,2,0:T(8,128)}, u32[]{:S(2)}, u32[]{:S(2)}) collective-permute-start(f32[5,2,128]{1,2,0:T(8,128)} %rev.37), channel_id=1, source_target_pairs={{0,1},{1,0},{2,3},{3,2},{4,5},{5,4},{6,7},{7,6},{8,9},{9,8},{10,11... | collective-permute-start | bytes 15368 | tf_op jit(solution)/shard_map/ppermute | solution.py:25
  20.5 10.8 %collective-permute-start.2 = (f32[4,2,128]{1,2,0:T(8,128)}, f32[4,2,128]{1,2,0:T(8,128)S(1)}, u32[]{:S(2)}, u32[]{:S(2)}) collective-permute-start(f32[4,2,128]{1,2,0:T(8,128)} %collective-permute-done.1), channel_id=1, source_target_pairs={{0,2},{1,3},{2,0},{3,1},{4,6},{5,7},{6,4},{7,5},{8,10},{9,11},{10,... | collective-permute-start | bytes 12296 | tf_op jit(solution)/shard_map/ppermute | solution.py:25
  29.4 14.0 %collective-permute-start.10 = (f32[5,2,128]{1,2,0:T(8,128)}, f32[5,2,128]{1,2,0:T(8,128)}, u32[]{:S(2)}, u32[]{:S(2)}) collective-permute-start(f32[5,2,128]{1,2,0:T(8,128)} %collective-permute-done.9), channel_id=1, source_target_pairs={{0,2},{1,3},{2,0},{3,1},{4,6},{5,7},{6,4},{7,5},{8,10},{9,11},{10,... | collective-permute-start | bytes 15368 | tf_op jit(solution)/shard_map/ppermute | solution.py:25
  31.3 16.2 %collective-permute-start.3 = (f32[4,2,128]{1,2,0:T(8,128)S(1)}, f32[4,2,128]{1,2,0:T(8,128)}, u32[]{:S(2)}, u32[]{:S(2)}) collective-permute-start(f32[4,2,128]{1,2,0:T(8,128)S(1)} %collective-permute-done.2), channel_id=1, source_target_pairs={{0,4},{1,5},{2,6},{3,7},{4,0},{5,1},{6,2},{7,3},{8,12},{9,13},{10,... | collective-permute-start | bytes 12296 | tf_op jit(solution)/shard_map/ppermute | solution.py:25
  43.4 30.6 %collective-permute-start.11 = (f32[5,2,128]{1,2,0:T(8,128)}, f32[5,2,128]{1,2,0:T(8,128)}, u32[]{:S(2)}, u32[]{:S(2)}) collective-permute-start(f32[5,2,128]{1,2,0:T(8,128)} %collective-permute-done.10), channel_id=1, source_target_pairs={{0,4},{1,5},{2,6},{3,7},{4,0},{5,1},{6,2},{7,3},{8,12},{9,13},{10,... | collective-permute-start | bytes 15368 | tf_op jit(solution)/shard_map/ppermute | solution.py:25
  47.5 32.8 %collective-permute-start.4 = (f32[4,2,128]{1,2,0:T(8,128)}, f32[4,2,128]{1,2,0:T(8,128)}, u32[]{:S(2)}, u32[]{:S(2)}) collective-permute-start(f32[4,2,128]{1,2,0:T(8,128)} %collective-permute-done.3), channel_id=1, source_target_pairs={{0,8},{1,9},{2,10},{3,11},{4,12},{5,13},{6,14},{7,15},{8,0},{9,1},... | collective-permute-start | bytes 12296 | tf_op jit(solution)/shard_map/ppermute | solution.py:25
  51.5 45.7 %collective-permute-start.13 = (f32[5,2,128]{1,2,0:T(8,128)}, f32[5,2,128]{1,2,0:T(8,128)}, u32[]{:S(2)}, u32[]{:S(2)}) collective-permute-start(f32[5,2,128]{1,2,0:T(8,128)} %get-tuple-element.110), channel_id=1, source_target_pairs={{16,0},{32,16},{48,32},{64,48},{80,64},{96,80},{112,96},{128,112},... | collective-permute-start | bytes 15368 | tf_op jit(solution)/shard_map/ppermute | solution.py:38
  74.0 20.4 %collective-permute-start.12 = (f32[5,2,128]{1,2,0:T(8,128)}, f32[5,2,128]{1,2,0:T(8,128)}, u32[]{:S(2)}, u32[]{:S(2)}) collective-permute-start(f32[5,2,128]{1,2,0:T(8,128)} %collective-permute-done.11), channel_id=1, source_target_pairs={{0,8},{1,9},{2,10},{3,11},{4,12},{5,13},{6,14},{7,15},{8,0},{9,1},... | collective-permute-start | bytes 15368 | tf_op jit(solution)/shard_map/ppermute | solution.py:25
  82.4 21.8 %collective-permute-start.7 = (f32[4,228,2]{1,2,0:T(2,128)}, f32[4,228,2]{1,2,0:T(2,128)S(1)}, u32[]{:S(2)}, u32[]{:S(2)}) collective-permute-start(f32[4,228,2]{1,2,0:T(2,128)} %get-tuple-element.58), channel_id=1, source_target_pairs={{1,0},{2,1},{3,2},{4,3},{5,4},{6,5},{7,6},{8,7},{9,8},{10,9},{11,1... | collective-permute-start | bytes 21896 | tf_op jit(solution)/shard_map/ppermute | solution.py:38
  83.6 20.6 %collective-permute-start.6 = (f32[4,228,2]{1,2,0:T(2,128)}, f32[4,228,2]{1,2,0:T(2,128)}, u32[]{:S(2)}, u32[]{:S(2)}) collective-permute-start(f32[4,228,2]{1,2,0:T(2,128)} %get-tuple-element.57), channel_id=1, source_target_pairs={{0,1},{1,2},{2,3},{3,4},{4,5},{5,6},{6,7},{7,8},{8,9},{9,10},{10,1... | collective-permute-start | bytes 21896 | tf_op jit(solution)/shard_map/ppermute | solution.py:36
  132.4 14.4 %collective-permute-start.19 = (f32[5,2,128]{1,2,0:T(8,128)S(1)}, f32[5,2,128]{1,2,0:T(8,128)S(1)}, u32[]{:S(2)}, u32[]{:S(2)}) collective-permute-start(f32[5,2,128]{1,2,0:T(8,128)S(1)} %collective-permute-done.18), channel_id=1, source_target_pairs={{0,4},{1,5},{2,6},{3,7},{4,0},{5,1},{6,2},{7,3},{8,12},{9,13},{10,... | collective-permute-start | bytes 15368 | tf_op jit(solution)/shard_map/ppermute | solution.py:25
  146.8 17.8 %collective-permute-start.20 = (f32[5,2,128]{1,2,0:T(8,128)S(1)}, f32[5,2,128]{1,2,0:T(8,128)}, u32[]{:S(2)}, u32[]{:S(2)}) collective-permute-start(f32[5,2,128]{1,2,0:T(8,128)S(1)} %collective-permute-done.19), channel_id=1, source_target_pairs={{0,8},{1,9},{2,10},{3,11},{4,12},{5,13},{6,14},{7,15},{8,0},{9,1},... | collective-permute-start | bytes 15368 | tf_op jit(solution)/shard_map/ppermute | solution.py:25
  148.5 19.5 %collective-permute-start.16 = (f32[5,2,128]{1,2,0:T(8,128)S(1)}, f32[5,2,128]{1,2,0:T(8,128)}, u32[]{:S(2)}, u32[]{:S(2)}) collective-permute-start(f32[5,2,128]{1,2,0:T(8,128)S(1)} %get-tuple-element.107), channel_id=1, source_target_pairs={{0,16},{16,32},{32,48},{48,64},{64,80},{80,96},{96,112},{112,128},... | collective-permute-start | bytes 15368 | tf_op jit(solution)/shard_map/ppermute | solution.py:36
  150.4 16.4 %collective-permute-start.21 = (f32[5,2,128]{1,2,0:T(8,128)}, f32[5,2,128]{1,2,0:T(8,128)}, u32[]{:S(2)}, u32[]{:S(2)}) collective-permute-start(f32[5,2,128]{1,2,0:T(8,128)} %get-tuple-element.108), channel_id=1, source_target_pairs={{16,0},{32,16},{48,32},{64,48},{80,64},{96,80},{112,96},{128,112},... | collective-permute-start | bytes 15368 | tf_op jit(solution)/shard_map/ppermute | solution.py:38
  199.9 13.0 %collective-permute-start.27 = (f32[5,2,128]{1,2,0:T(8,128)}, f32[5,2,128]{1,2,0:T(8,128)}, u32[]{:S(2)}, u32[]{:S(2)}) collective-permute-start(f32[5,2,128]{1,2,0:T(8,128)} %collective-permute-done.26), channel_id=1, source_target_pairs={{0,4},{1,5},{2,6},{3,7},{4,0},{5,1},{6,2},{7,3},{8,12},{9,13},{10,... | collective-permute-start | bytes 15368 | tf_op jit(solution)/shard_map/ppermute | solution.py:25
  212.9 30.4 %collective-permute-start.28 = (f32[5,2,128]{1,2,0:T(8,128)}, f32[5,2,128]{1,2,0:T(8,128)}, u32[]{:S(2)}, u32[]{:S(2)}) collective-permute-start(f32[5,2,128]{1,2,0:T(8,128)} %collective-permute-done.27), channel_id=1, source_target_pairs={{0,8},{1,9},{2,10},{3,11},{4,12},{5,13},{6,14},{7,15},{8,0},{9,1},... | collective-permute-start | bytes 15368 | tf_op jit(solution)/shard_map/ppermute | solution.py:25
  218.6 19.4 %collective-permute-start.43 = (f32[3,2,128]{1,2,0:T(8,128)S(1)}, f32[3,2,128]{1,2,0:T(8,128)}, u32[]{:S(2)}, u32[]{:S(2)}) collective-permute-start(f32[3,2,128]{1,2,0:T(8,128)S(1)} %collective-permute-done.42), channel_id=1, source_target_pairs={{0,4},{1,5},{2,6},{3,7},{4,0},{5,1},{6,2},{7,3},{8,12},{9,13},{10,... | collective-permute-start | bytes 9224 | tf_op jit(solution)/shard_map/ppermute | solution.py:25
  224.0 49.0 %collective-permute-start.40 = (f32[3,2,128]{1,2,0:T(8,128)}, f32[3,2,128]{1,2,0:T(8,128)}, u32[]{:S(2)}, u32[]{:S(2)}) collective-permute-start(f32[3,2,128]{1,2,0:T(8,128)} %get-tuple-element.144), channel_id=1, source_target_pairs={{0,16},{16,32},{32,48},{48,64},{64,80},{80,96},{96,112},{112,128},... | collective-permute-start | bytes 9224 | tf_op jit(solution)/shard_map/ppermute | solution.py:36
  226.0 32.5 %collective-permute-start.45 = (f32[3,2,128]{1,2,0:T(8,128)}, f32[3,2,128]{1,2,0:T(8,128)}, u32[]{:S(2)}, u32[]{:S(2)}) collective-permute-start(f32[3,2,128]{1,2,0:T(8,128)} %get-tuple-element.145), channel_id=1, source_target_pairs={{16,0},{32,16},{48,32},{64,48},{80,64},{96,80},{112,96},{128,112},... | collective-permute-start | bytes 9224 | tf_op jit(solution)/shard_map/ppermute | solution.py:38
  238.0 20.5 %collective-permute-start.44 = (f32[3,2,128]{1,2,0:T(8,128)}, f32[3,2,128]{1,2,0:T(8,128)}, u32[]{:S(2)}, u32[]{:S(2)}) collective-permute-start(f32[3,2,128]{1,2,0:T(8,128)} %collective-permute-done.43), channel_id=1, source_target_pairs={{0,8},{1,9},{2,10},{3,11},{4,12},{5,13},{6,14},{7,15},{8,0},{9,1},... | collective-permute-start | bytes 9224 | tf_op jit(solution)/shard_map/ppermute | solution.py:25
  241.5 14.0 %collective-permute-start.24 = (f32[5,2,128]{1,2,0:T(8,128)S(1)}, f32[5,2,128]{1,2,0:T(8,128)}, u32[]{:S(2)}, u32[]{:S(2)}) collective-permute-start(f32[5,2,128]{1,2,0:T(8,128)S(1)} %get-tuple-element.105), channel_id=1, source_target_pairs={{0,16},{16,32},{32,48},{48,64},{64,80},{80,96},{96,112},{112,128},... | collective-permute-start | bytes 15368 | tf_op jit(solution)/shard_map/ppermute | solution.py:36
  243.4 10.9 %collective-permute-start.29 = (f32[5,2,128]{1,2,0:T(8,128)}, f32[5,2,128]{1,2,0:T(8,128)}, u32[]{:S(2)}, u32[]{:S(2)}) collective-permute-start(f32[5,2,128]{1,2,0:T(8,128)} %get-tuple-element.106), channel_id=1, source_target_pairs={{16,0},{32,16},{48,32},{64,48},{80,64},{96,80},{112,96},{128,112},... | collective-permute-start | bytes 15368 | tf_op jit(solution)/shard_map/ppermute | solution.py:38
  273.1 10.1 %collective-permute-start.33 = (f32[5,2,128]{1,2,0:T(8,128)}, f32[5,2,128]{1,2,0:T(8,128)S(1)}, u32[]{:S(2)}, u32[]{:S(2)}) collective-permute-start(f32[5,2,128]{1,2,0:T(8,128)} %rev.40), channel_id=1, source_target_pairs={{0,1},{1,0},{2,3},{3,2},{4,5},{5,4},{6,7},{7,6},{8,9},{9,8},{10,11... | collective-permute-start | bytes 15368 | tf_op jit(solution)/shard_map/ppermute | solution.py:25
  273.9 18.8 %collective-permute-start.47 = (f32[3,228,2]{1,2,0:T(2,128)S(1)}, f32[3,228,2]{1,2,0:T(2,128)S(1)}, u32[]{:S(2)}, u32[]{:S(2)}) collective-permute-start(f32[3,228,2]{1,2,0:T(2,128)S(1)} %get-tuple-element.82), channel_id=1, source_target_pairs={{1,0},{2,1},{3,2},{4,3},{5,4},{6,5},{7,6},{8,7},{9,8},{10,9},{11,1... | collective-permute-start | bytes 16424 | tf_op jit(solution)/shard_map/ppermute | solution.py:38
  274.0 18.7 %collective-permute-start.46 = (f32[3,228,2]{1,2,0:T(2,128)S(1)}, f32[3,228,2]{1,2,0:T(2,128)S(1)}, u32[]{:S(2)}, u32[]{:S(2)}) collective-permute-start(f32[3,228,2]{1,2,0:T(2,128)S(1)} %get-tuple-element.81), channel_id=1, source_target_pairs={{0,1},{1,2},{2,3},{3,4},{4,5},{5,6},{6,7},{7,8},{8,9},{9,10},{10,1... | collective-permute-start | bytes 16424 | tf_op jit(solution)/shard_map/ppermute | solution.py:36
  292.0 15.9 %collective-permute-start.35 = (f32[5,2,128]{1,2,0:T(8,128)S(1)}, f32[5,2,128]{1,2,0:T(8,128)S(1)}, u32[]{:S(2)}, u32[]{:S(2)}) collective-permute-start(f32[5,2,128]{1,2,0:T(8,128)S(1)} %collective-permute-done.34), channel_id=1, source_target_pairs={{0,4},{1,5},{2,6},{3,7},{4,0},{5,1},{6,2},{7,3},{8,12},{9,13},{10,... | collective-permute-start | bytes 15368 | tf_op jit(solution)/shard_map/ppermute | solution.py:25
  307.9 20.1 %collective-permute-start.36 = (f32[5,2,128]{1,2,0:T(8,128)S(1)}, f32[5,2,128]{1,2,0:T(8,128)}, u32[]{:S(2)}, u32[]{:S(2)}) collective-permute-start(f32[5,2,128]{1,2,0:T(8,128)S(1)} %collective-permute-done.35), channel_id=1, source_target_pairs={{0,8},{1,9},{2,10},{3,11},{4,12},{5,13},{6,14},{7,15},{8,0},{9,1},... | collective-permute-start | bytes 15368 | tf_op jit(solution)/shard_map/ppermute | solution.py:25
  313.4 18.1 %collective-permute-start.32 = (f32[5,2,128]{1,2,0:T(8,128)S(1)}, f32[5,2,128]{1,2,0:T(8,128)}, u32[]{:S(2)}, u32[]{:S(2)}) collective-permute-start(f32[5,2,128]{1,2,0:T(8,128)S(1)} %copy-done), channel_id=1, source_target_pairs={{0,16},{16,32},{32,48},{48,64},{64,80},{80,96},{96,112},{112,128},... | collective-permute-start | bytes 15368 | tf_op jit(solution)/shard_map/ppermute | solution.py:36
  315.3 15.0 %collective-permute-start.37 = (f32[5,2,128]{1,2,0:T(8,128)}, f32[5,2,128]{1,2,0:T(8,128)}, u32[]{:S(2)}, u32[]{:S(2)}) collective-permute-start(f32[5,2,128]{1,2,0:T(8,128)} %get-tuple-element.104), channel_id=1, source_target_pairs={{16,0},{32,16},{48,32},{64,48},{80,64},{96,80},{112,96},{128,112},... | collective-permute-start | bytes 15368 | tf_op jit(solution)/shard_map/ppermute | solution.py:38
  358.2 11.7 %collective-permute-start.51 = (f32[3,2,128]{1,2,0:T(8,128)S(1)}, f32[3,2,128]{1,2,0:T(8,128)S(1)}, u32[]{:S(2)}, u32[]{:S(2)}) collective-permute-start(f32[3,2,128]{1,2,0:T(8,128)S(1)} %collective-permute-done.50), channel_id=1, source_target_pairs={{0,4},{1,5},{2,6},{3,7},{4,0},{5,1},{6,2},{7,3},{8,12},{9,13},{10,... | collective-permute-start | bytes 9224 | tf_op jit(solution)/shard_map/ppermute | solution.py:25
  358.2 13.6 %collective-permute-start.53 = (f32[3,2,128]{1,2,0:T(8,128)S(1)}, f32[3,2,128]{1,2,0:T(8,128)S(1)}, u32[]{:S(2)}, u32[]{:S(2)}) collective-permute-start(f32[3,2,128]{1,2,0:T(8,128)S(1)} %get-tuple-element.143), channel_id=1, source_target_pairs={{16,0},{32,16},{48,32},{64,48},{80,64},{96,80},{112,96},{128,112},... | collective-permute-start | bytes 9224 | tf_op jit(solution)/shard_map/ppermute | solution.py:38
  369.9 9.6 %collective-permute-start.52 = (f32[3,2,128]{1,2,0:T(8,128)S(1)}, f32[3,2,128]{1,2,0:T(8,128)S(1)}, u32[]{:S(2)}, u32[]{:S(2)}) collective-permute-start(f32[3,2,128]{1,2,0:T(8,128)S(1)} %collective-permute-done.51), channel_id=1, source_target_pairs={{0,8},{1,9},{2,10},{3,11},{4,12},{5,13},{6,14},{7,15},{8,0},{9,1},... | collective-permute-start | bytes 9224 | tf_op jit(solution)/shard_map/ppermute | solution.py:25
  369.9 9.9 %collective-permute-start.48 = (f32[3,2,128]{1,2,0:T(8,128)S(1)}, f32[3,2,128]{1,2,0:T(8,128)S(1)}, u32[]{:S(2)}, u32[]{:S(2)}) collective-permute-start(f32[3,2,128]{1,2,0:T(8,128)S(1)} %get-tuple-element.142), channel_id=1, source_target_pairs={{0,16},{16,32},{32,48},{48,64},{64,80},{80,96},{96,112},{112,128},... | collective-permute-start | bytes 9224 | tf_op jit(solution)/shard_map/ppermute | solution.py:36
  400.2 23.8 %collective-permute-start.61 = (f32[3,2,128]{1,2,0:T(8,128)S(1)}, f32[3,2,128]{1,2,0:T(8,128)S(1)}, u32[]{:S(2)}, u32[]{:S(2)}) collective-permute-start(f32[3,2,128]{1,2,0:T(8,128)S(1)} %get-tuple-element.141), channel_id=1, source_target_pairs={{16,0},{32,16},{48,32},{64,48},{80,64},{96,80},{112,96},{128,112},... | collective-permute-start | bytes 9224 | tf_op jit(solution)/shard_map/ppermute | solution.py:38
  407.9 17.8 %collective-permute-start.60 = (f32[3,2,128]{1,2,0:T(8,128)S(1)}, f32[3,2,128]{1,2,0:T(8,128)S(1)}, u32[]{:S(2)}, u32[]{:S(2)}) collective-permute-start(f32[3,2,128]{1,2,0:T(8,128)S(1)} %collective-permute-done.59), channel_id=1, source_target_pairs={{0,8},{1,9},{2,10},{3,11},{4,12},{5,13},{6,14},{7,15},{8,0},{9,1},... | collective-permute-start | bytes 9224 | tf_op jit(solution)/shard_map/ppermute | solution.py:25
  452.0 16.2 %collective-permute-start.67 = (f32[3,2,128]{1,2,0:T(8,128)S(1)}, f32[3,2,128]{1,2,0:T(8,128)S(1)}, u32[]{:S(2)}, u32[]{:S(2)}) collective-permute-start(f32[3,2,128]{1,2,0:T(8,128)S(1)} %collective-permute-done.66), channel_id=1, source_target_pairs={{0,4},{1,5},{2,6},{3,7},{4,0},{5,1},{6,2},{7,3},{8,12},{9,13},{10,... | collective-permute-start | bytes 9224 | tf_op jit(solution)/shard_map/ppermute | solution.py:25
  452.0 18.1 %collective-permute-start.69 = (f32[3,2,128]{1,2,0:T(8,128)S(1)}, f32[3,2,128]{1,2,0:T(8,128)S(1)}, u32[]{:S(2)}, u32[]{:S(2)}) collective-permute-start(f32[3,2,128]{1,2,0:T(8,128)S(1)} %get-tuple-element.139), channel_id=1, source_target_pairs={{16,0},{32,16},{48,32},{64,48},{80,64},{96,80},{112,96},{128,112},... | collective-permute-start | bytes 9224 | tf_op jit(solution)/shard_map/ppermute | solution.py:38
  468.2 9.6 %collective-permute-start.68 = (f32[3,2,128]{1,2,0:T(8,128)S(1)}, f32[3,2,128]{1,2,0:T(8,128)S(1)}, u32[]{:S(2)}, u32[]{:S(2)}) collective-permute-start(f32[3,2,128]{1,2,0:T(8,128)S(1)} %collective-permute-done.67), channel_id=1, source_target_pairs={{0,8},{1,9},{2,10},{3,11},{4,12},{5,13},{6,14},{7,15},{8,0},{9,1},... | collective-permute-start | bytes 9224 | tf_op jit(solution)/shard_map/ppermute | solution.py:25
  468.2 9.9 %collective-permute-start.64 = (f32[3,2,128]{1,2,0:T(8,128)S(1)}, f32[3,2,128]{1,2,0:T(8,128)S(1)}, u32[]{:S(2)}, u32[]{:S(2)}) collective-permute-start(f32[3,2,128]{1,2,0:T(8,128)S(1)} %get-tuple-element.138), channel_id=1, source_target_pairs={{0,16},{16,32},{32,48},{48,64},{64,80},{80,96},{96,112},{112,128},... | collective-permute-start | bytes 9224 | tf_op jit(solution)/shard_map/ppermute | solution.py:36
  496.9 24.2 %collective-permute-start.77 = (f32[3,2,128]{1,2,0:T(8,128)S(1)}, f32[3,2,128]{1,2,0:T(8,128)S(1)}, u32[]{:S(2)}, u32[]{:S(2)}) collective-permute-start(f32[3,2,128]{1,2,0:T(8,128)S(1)} %get-tuple-element.137), channel_id=1, source_target_pairs={{16,0},{32,16},{48,32},{64,48},{80,64},{96,80},{112,96},{128,112},... | collective-permute-start | bytes 9224 | tf_op jit(solution)/shard_map/ppermute | solution.py:38
  504.8 18.0 %collective-permute-start.76 = (f32[3,2,128]{1,2,0:T(8,128)S(1)}, f32[3,2,128]{1,2,0:T(8,128)S(1)}, u32[]{:S(2)}, u32[]{:S(2)}) collective-permute-start(f32[3,2,128]{1,2,0:T(8,128)S(1)} %collective-permute-done.75), channel_id=1, source_target_pairs={{0,8},{1,9},{2,10},{3,11},{4,12},{5,13},{6,14},{7,15},{8,0},{9,1},... | collective-permute-start | bytes 9224 | tf_op jit(solution)/shard_map/ppermute | solution.py:25
  548.2 16.5 %collective-permute-start.83 = (f32[3,2,128]{1,2,0:T(8,128)S(1)}, f32[3,2,128]{1,2,0:T(8,128)S(1)}, u32[]{:S(2)}, u32[]{:S(2)}) collective-permute-start(f32[3,2,128]{1,2,0:T(8,128)S(1)} %collective-permute-done.82), channel_id=1, source_target_pairs={{0,4},{1,5},{2,6},{3,7},{4,0},{5,1},{6,2},{7,3},{8,12},{9,13},{10,... | collective-permute-start | bytes 9224 | tf_op jit(solution)/shard_map/ppermute | solution.py:25
  548.6 18.1 %collective-permute-start.85 = (f32[3,2,128]{1,2,0:T(8,128)S(1)}, f32[3,2,128]{1,2,0:T(8,128)S(1)}, u32[]{:S(2)}, u32[]{:S(2)}) collective-permute-start(f32[3,2,128]{1,2,0:T(8,128)S(1)} %get-tuple-element.135), channel_id=1, source_target_pairs={{16,0},{32,16},{48,32},{64,48},{80,64},{96,80},{112,96},{128,112},... | collective-permute-start | bytes 9224 | tf_op jit(solution)/shard_map/ppermute | solution.py:38
  564.7 9.6 %collective-permute-start.84 = (f32[3,2,128]{1,2,0:T(8,128)S(1)}, f32[3,2,128]{1,2,0:T(8,128)S(1)}, u32[]{:S(2)}, u32[]{:S(2)}) collective-permute-start(f32[3,2,128]{1,2,0:T(8,128)S(1)} %collective-permute-done.83), channel_id=1, source_target_pairs={{0,8},{1,9},{2,10},{3,11},{4,12},{5,13},{6,14},{7,15},{8,0},{9,1},... | collective-permute-start | bytes 9224 | tf_op jit(solution)/shard_map/ppermute | solution.py:25
  564.8 9.8 %collective-permute-start.80 = (f32[3,2,128]{1,2,0:T(8,128)S(1)}, f32[3,2,128]{1,2,0:T(8,128)S(1)}, u32[]{:S(2)}, u32[]{:S(2)}) collective-permute-start(f32[3,2,128]{1,2,0:T(8,128)S(1)} %get-tuple-element.134), channel_id=1, source_target_pairs={{0,16},{16,32},{32,48},{48,64},{64,80},{80,96},{96,112},{112,128},... | collective-permute-start | bytes 9224 | tf_op jit(solution)/shard_map/ppermute | solution.py:36
  (60 other events, 345.6 us)
where the time goes:
time: 592 us; the launch traced here: 583 us
  waiting for transfers between devices  339 us (57%)
  starting transfers between devices  166 us (28%)
  local copies, waits for them, and re-layouts  39.1 us (7%)
  other arithmetic  31.8 us (5%)
    ppermute x44, waiting for transfers between devices, from_partner(): return lax.ppermute(value, axis, pairs)  289 us
    ppermute x44, starting transfers between devices, from_partner(): return lax.ppermute(value, axis, pairs)  72.3 us
    ppermute x22, starting transfers between devices, extended_2(): lax.ppermute(head, axis, [((i + 1) % count, i) for i in range(ends)])  56.2 us
    ppermute x22, waiting for transfers between devices, extended_2(): lax.ppermute(tail, axis, [(i, (i + 1) % count) for i in range(ends)])  38.1 us
    ppermute x22, starting transfers between devices, extended_2(): lax.ppermute(tail, axis, [(i, (i + 1) % count) for i in range(ends)])  37.1 us
    rev x11, local copies, waits for them, and re-layouts, extend(): flipped = jnp.flip(field_stack[:, -2:, :], axis=1)  14.1 us
    ppermute x22, waiting for transfers between devices, extended_2(): lax.ppermute(head, axis, [((i + 1) % count, i) for i in range(ends)])  12.3 us
  transfers between devices with their start and end apart: 88, of which 59 were waited for; matrix products, arithmetic and copies ran while one was open for 8% of the time, Pallas kernels for 0%

commit v1 on v0

v1 whole, which is shorter than its diff:
```python
import math

import jax
import jax.numpy as jnp
from jax import lax
from jax.experimental import pallas as pl
from jax.experimental.pallas import tpu as pltpu
from jax.sharding import PartitionSpec as P

ICE_GROUPS = (2, 2)
SEA_GROUPS = (3, 3)
EDGE = 16
ICE_CHUNK = 24
SEA_CHUNK = 24
LANES = 128
MESH_ID = pl.DeviceIdType.MESH

U, V, S1, S2, S12, STRENGTH, MASSX, COVER, WX, WY, OU, OV = range(12)
C1, C2, RELAX, INVM, KU, KV = range(6)
LEVEL, TU, TV, DEPTH, LAND, SX, SY = range(7)
ICE_SIGNS = {U: -1.0, V: -1.0}
SEA_SIGNS = {TU: -1.0, TV: -1.0}


class Exchange:
    def __init__(self, name, fields, steps, rows):
        self.name, self.fields, self.steps = name, fields, steps
        self.width = 2 * steps
        self.groups = 4 if len(fields) * self.width <= 32 else 2
        self.group_lanes = LANES // self.groups
        assert len(fields) * self.width <= self.group_lanes
        self.group_rows = rows // self.groups
        self.extra = name == "ice0"
        count = len(fields) * self.width + (1 if self.extra else 0)
        self.strip_rows = -(-count // 8) * 8

    def scratch(self, blocks):
        f32 = jnp.float32
        packed, got = (self.group_rows, LANES), (self.group_rows + 16, LANES)
        strip = (self.strip_rows, LANES)
        return dict(
            top=pltpu.VMEM(strip, f32),
            bot=pltpu.VMEM(strip, f32),
            low=pltpu.VMEM(strip, f32),
            high=pltpu.VMEM(strip, f32),
            west=pltpu.VMEM(packed, f32),
            east=pltpu.VMEM(packed, f32),
            right=pltpu.VMEM(got, f32),
            left=pltpu.VMEM(got, f32),
            strips=pltpu.VMEM((blocks * self.strip_rows, LANES), f32),
            send=pltpu.SemaphoreType.DMA((8,)),
            recv=pltpu.SemaphoreType.DMA((8,)),
            strip_send=pltpu.SemaphoreType.DMA((blocks,)),
            strip_recv=pltpu.SemaphoreType.DMA((blocks,)),
        )


def plan(rows):
    ice = [Exchange(f"ice{i}", list(range(12 if i == 0 else 5)), s, rows) for i, s in enumerate(ICE_GROUPS)]
    first = Exchange("sea0", [LEVEL, TU, TV, DEPTH, LAND], SEA_GROUPS[0], rows)
    surf = Exchange("surf", [SX, SY], SEA_GROUPS[0], rows)
    later = [Exchange(f"sea{i}", [LEVEL, TU, TV], s, rows) for i, s in enumerate(SEA_GROUPS) if i]
    return ice, first, surf, later


def kernel_body(
    blocks,
    bands,
    names,
    vel_in,
    str_in,
    mass_in,
    strength_in,
    wind_in,
    level_in,
    trans_in,
    depth_in,
    land_in,
    icemask_in,
    partner_in,
    vel_out,
    str_out,
    level_out,
    trans_out,
    *scratch,
):
    ref = dict(zip(names, scratch))
    ice, der, sea, cor = ref["ice"], ref["der"], ref["sea"], ref["cor"]
    ist, ider, sst, sder = ref["ist"], ref["ider"], ref["sst"], ref["sder"]
    masks, partner, perm = ref["masks"], ref["partner"], ref["perm"]
    in_sem, out_sem = ref["in_sem"], ref["out_sem"]
    rows = mass_in.shape[0]
    total_rows = rows * bands
    own = slice(EDGE, EDGE + rows)
    full = rows + 16
    gy, gx = lax.axis_index("gy"), lax.axis_index("gx")
    west_x, east_x = lax.rem(gx + blocks - 1, blocks), lax.rem(gx + 1, blocks)
    is_top, is_low = gy == bands - 1, gy == 0
    ice_ex, sea_ex, surf_ex, later_ex = plan(rows)

    barrier = pltpu.get_barrier_semaphore()

    def greet(y, x):
        pl.semaphore_signal(barrier, inc=1, device_id=(y, x), device_id_type=MESH_ID)

    greet(gy, west_x)
    greet(gy, east_x)

    @pl.when(gy < bands - 1)
    def _():
        for x in (gx, west_x, east_x):
            greet(gy + 1, x)

    @pl.when(gy > 0)
    def _():
        for x in (gx, west_x, east_x):
            greet(gy - 1, x)

    @pl.when(is_top)
    def _():
        def one(j, carry):
            greet(gy, lax.rem(gx + j, blocks))
            return carry

        lax.fori_loop(1, blocks, one, 0)

    loads = [
        (vel_in, ice.at[U : V + 1, 0, own]),
        (str_in, ice.at[S1 : S12 + 1, 0, own]),
        (mass_in, ice.at[MASSX, 0, own]),
        (strength_in, ice.at[STRENGTH, 0, own]),
        (wind_in, ice.at[WX : WY + 1, 0, own]),
        (level_in, sea.at[LEVEL, 0, own]),
        (trans_in, sea.at[TU : TV + 1, 0, own]),
        (depth_in, sea.at[DEPTH, 0, own]),
        (land_in, masks.at[0]),
        (icemask_in, masks.at[1]),
        (partner_in, partner),
    ]
    loads = [pltpu.make_async_copy(a, b, in_sem.at[i]) for i, (a, b) in enumerate(loads)]
    for copy in loads:
        copy.start()

    def loop(count, body):
        def one(i, carry):
            body(i)
            return carry

        lax.fori_loop(0, count, one, 0)

    def coriolis(i):
        at = pl.multiple_of(i * 8, 8)
        r = lax.broadcasted_iota(jnp.int32, (8, LANES), 0) + (gy * rows + at - EDGE)
        angle = jnp.pi * ((r.astype(jnp.float32) + 0.5) / total_rows - 0.5)
        cor[pl.ds(at, 8), :] = 0.5 * jnp.sin(angle)

    loop((rows + 2 * EDGE) // 8, coriolis)
    for copy in loads:
        copy.wait()

    def prepare(i):
        at = pl.multiple_of(i * 8, 8)
        here, m = pl.ds(at + EDGE, 8), pl.ds(at, 8)
        land = masks[0, m, :].astype(jnp.float32)
        cover = land * masks[1, m, :].astype(jnp.float32)
        depth = sea[DEPTH, 0, here, :]
        sea[LAND, 0, here, :] = land
        ice[COVER, 0, here, :] = cover
        ice[MASSX, 0, here, :] = ice[MASSX, 0, here, :] + 1.0 - cover
        ice[OU, 0, here, :] = sea[TU, 0, here, :] / depth
        ice[OV, 0, here, :] = sea[TV, 0, here, :] / depth

    loop(rows // 8, prepare)

    lane8 = lax.broadcasted_iota(jnp.int32, (8, LANES), 1)

    def stage(ex, store):
        w = ex.width
        top, bot = ref[ex.name, "top"], ref[ex.name, "bot"]
        for k, f in enumerate(ex.fields):
            top[k * w : (k + 1) * w, :] = store[f, 0, EDGE + rows - w : EDGE + rows, :]
            bot[k * w : (k + 1) * w, :] = store[f, 0, EDGE : EDGE + w, :]
        if ex.extra:
            at = len(ex.fields) * w
            local = partner[...] - (blocks - 1 - gx) * LANES
            top[at : at + 1, :] = local.astype(jnp.float32)

        def pack(i):
            to_west = to_east = None
            for g in range(ex.groups):
                for k, f in enumerate(ex.fields):
                    at = g * ex.group_lanes + k * w
                    here = pl.ds(pl.multiple_of(EDGE + g * ex.group_rows + i * 8, 8), 8)
                    x = store[f, 0, here, :]
                    a = pltpu.roll(x, at, 1) if at else x
                    b = pltpu.roll(x, (at + w) % LANES, 1) if (at + w) % LANES else x
                    if to_west is None:
                        to_west, to_east = a, b
                    else:
                        keep = lane8 < at
                        to_west = jnp.where(keep, to_west, a)
                        to_east = jnp.where(keep, to_east, b)
            m = pl.ds(pl.multiple_of(i * 8, 8), 8)
            ref[ex.name, "west"][m, :] = to_west
            ref[ex.name, "east"][m, :] = to_east

        loop(ex.group_rows // 8, pack)

    def sends(ex):
        r = lambda part: ref[ex.name, part]
        n = ex.group_rows
        last, first = pl.ds(n - 8, 8), pl.ds(0, 8)
        mid, low, high = pl.ds(0, n), pl.ds(n, 8), pl.ds(n + 8, 8)
        up, down, flat = 1, -1, 0
        table = [
            (r("top"), r("low"), up, gx),
            (r("bot"), r("high"), down, gx),
            (r("west"), r("right").at[mid], flat, west_x),
            (r("east"), r("left").at[mid], flat, east_x),
            (r("west").at[last], r("right").at[low], up, west_x),
            (r("east").at[last], r("left").at[low], up, east_x),
            (r("west").at[first], r("right").at[high], down, west_x),
            (r("east").at[first], r("left").at[high], down, east_x),
        ]
        out = []
        for i, (src, dst, dy, x) in enumerate(table):
            copy = pltpu.make_async_remote_copy(
                src_ref=src,
                dst_ref=dst,
                send_sem=r("send").at[i],
                recv_sem=r("recv").at[i],
                device_id=(gy + dy, x),
                device_id_type=MESH_ID,
            )
            out.append((dy, copy))
        return out

    def strip_copy(ex, target, source):
        n = ex.strip_rows
        return pltpu.make_async_remote_copy(
            src_ref=ref[ex.name, "top"],
            dst_ref=ref[ex.name, "strips"].at[pl.ds(pl.multiple_of(source * n, 8), n)],
            send_sem=ref[ex.name, "strip_send"].at[target],
            recv_sem=ref[ex.name, "strip_recv"].at[source],
            device_id=(gy, target),
            device_id_type=MESH_ID,
        )

    def each_strip(ex, action):
        reach = ex.steps

        @pl.when(is_top)
        def _():
            def one(j, carry):
                x = lax.rem(gx + j, blocks)
                gap = lax.rem(x + gx + 1, blocks)
                near = (j <= reach) | (j >= blocks - reach) | (gap <= reach) | (gap >= blocks - reach)

                @pl.when(near)
                def _():
                    action(x)

                return carry

            lax.fori_loop(1, blocks, one, 0)

    def start(ex):
        each_strip(ex, lambda x: strip_copy(ex, x, gx).start())
        copies = sends(ex)
        for dy in (0, 1, -1):
            chosen = [c for d, c in copies if d == dy]

            def go(chosen=chosen):
                for c in chosen:
                    c.start()

            if dy == 0:
                go()
            else:
                pl.when((gy < bands - 1) if dy > 0 else (gy > 0))(go)
        n = ex.strip_rows

        @pl.when(is_top)
        def _():
            ref[ex.name, "strips"][pl.ds(pl.multiple_of(gx * n, 8), n), :] = ref[ex.name, "top"][...]

    def wait_recv(ex):
        copies = sends(ex)
        for dy in (0, 1, -1):
            chosen = [c for d, c in copies if d == dy]

            def go(chosen=chosen):
                for c in chosen:
                    c.wait_recv()

            if dy == 0:
                go()
            else:
                pl.when((gy > 0) if dy > 0 else (gy < bands - 1))(go)

    def wait_strips(ex):
        each_strip(ex, lambda x: strip_copy(ex, gx, x).wait_recv())

    def wait_send(ex):
        copies = sends(ex)
        for dy in (0, 1, -1):
            chosen = [c for d, c in copies if d == dy]

            def go(chosen=chosen):
                for c in chosen:
                    c.wait_send()

            if dy == 0:
                go()
            else:
                pl.when((gy < bands - 1) if dy > 0 else (gy > 0))(go)
        each_strip(ex, lambda x: strip_copy(ex, x, gx).wait_send())

    def unpack(ex, store, ones):
        w, n = ex.width, ex.group_rows
        right, left = ref[ex.name, "right"], ref[ex.name, "left"]

        def place(source, g, target):
            x, y = right[source, :], left[source, :]
            for k, f in enumerate(ex.fields):
                at = g * ex.group_lanes + k * w
                a = pltpu.roll(x, (LANES - at) % LANES, 1) if at else x
                shift = (2 * LANES - w - at) % LANES
                b = pltpu.roll(y, shift, 1) if shift else y
                store[f, 1, target, :] = jnp.where(lane8 < LANES // 2, a, b)

        def main(i):
            source = pl.ds(pl.multiple_of(i * 8, 8), 8)
            for g in range(ex.groups):
                place(source, g, pl.ds(pl.multiple_of(EDGE + g * n + i * 8, 8), 8))

        loop(n // 8, main)

        @pl.when(gy > 0)
        def _():
            place(pl.ds(n, 8), ex.groups - 1, pl.ds(EDGE - 8, 8))
            for k, f in enumerate(ex.fields):
                store[f, 0, EDGE - w : EDGE, :] = ref[ex.name, "low"][k * w : (k + 1) * w, :]

        @pl.when(gy < bands - 1)
        def _():
            place(pl.ds(n + 8, 8), 0, pl.ds(EDGE + rows, 8))
            for k, f in enumerate(ex.fields):
                store[f, 0, EDGE + rows : EDGE + rows + w, :] = ref[ex.name, "high"][k * w : (k + 1) * w, :]

        @pl.when(is_low)
        def _():
            for f in ex.fields:
                fill = jnp.full((8, LANES), 1.0 if f == ones else 0.0, jnp.float32)
                store[f, 0, EDGE - 8 : EDGE, :] = fill
                store[f, 1, EDGE - 8 : EDGE, :] = fill

    blane = lax.broadcasted_iota(jnp.int32, (blocks, LANES), 1)
    turn = 7 - lax.broadcasted_iota(jnp.int32, (8, LANES), 0)

    def strip_load(ex, strip):
        w, n = ex.width, ex.strip_rows
        got = ref[ex.name, "strips"]
        for k, f in enumerate(ex.fields):
            for d in range(w):
                strip[f, 2 + d] = got[pl.ds(k * w + w - 1 - d, blocks, stride=n), :]
        if ex.extra:
            perm[...] = got[pl.ds(len(ex.fields) * w, blocks, stride=n), :].astype(jnp.int32)

    def fold_rows(x):
        parts = [jnp.take_along_axis(x[b : b + 8], turn, axis=0) for b in range(blocks - 8, -1, -8)]
        index = perm[...]
        parts = [jnp.take_along_axis(p, index[8 * i : 8 * i + 8], axis=1) for i, p in enumerate(parts)]
        return jnp.concatenate(parts, axis=0)

    def fold(strip, store, fields, signs):
        for f in fields:
            for k in (0, 1):
                x = fold_rows(strip[f, 2 + k])
                strip[f, 1 - k] = -x if f in signs else x
        lane1 = lax.broadcasted_iota(jnp.int32, (1, LANES), 1)
        for f in fields:
            for k in (0, 1):
                row = slice(EDGE + rows + k, EDGE + rows + k + 1)
                store[f, 0, row, :] = strip[f, 1 - k, pl.ds(gx, 1), :]
                store[f, 1, row, :] = jnp.where(
                    lane1 < LANES // 2, strip[f, 1 - k, pl.ds(east_x, 1), :], strip[f, 1 - k, pl.ds(west_x, 1), :]
                )

    def dx_strip(x):
        a = jnp.where(blane == 0, pltpu.roll(x, blocks - 1, 0), x)
        b = jnp.where(blane == LANES - 1, pltpu.roll(x, 1, 0), x)
        return pltpu.roll(a, LANES - 1, 1) - pltpu.roll(b, 1, 1)

    def row_coriolis(i):
        row = total_rows + 1 - i
        return 0.5 * math.sin(math.pi * ((row + 0.5) / total_rows - 0.5))

    def ice_coefficients(strength, massx, cover, u, v, wx, wy):
        relax = 2.0 + jnp.sqrt(16.0 * strength / massx)
        share = cover / (1.0 + relax)
        inv = 1.0 / massx
        return share * relax, share * strength, relax, inv, u + wx * inv, v + wy * inv

    def stresses(exx, eyy, shear, c1, c2, s1, s2, s12):
        div, ten = exx + eyy, exx - eyy
        r = lax.rsqrt(div * div + (ten * ten + shear * shear) * 0.25 + 0.01)
        g = c2 * r
        return c1 * s1 + (g * div - c2), c1 * s2 + (0.25 * g) * ten, c1 * s12 + (0.125 * g) * shear

    def velocities(fx, fy, u, v, relax, inv, cover, ku, kv, ou, ov, f):
        rx, ry = ou - u, ov - v
        drag = 0.5 * jnp.sqrt(rx * rx + ry * ry)
        part = cover / (1.0 + relax + drag * inv)
        new_u = part * (relax * u + ku + inv * (fx + drag * ou) + f * v)
        new_v = part * (relax * v + kv + inv * (fy + drag * ov) - f * u)
        return new_u, new_v

    def dx_pair(m, h, first, last):
        am, ah = jnp.where(first, h, m), jnp.where(first, m, h)
        bm, bh = jnp.where(last, h, m), jnp.where(last, m, h)
        return (
            pltpu.roll(am, LANES - 1, 1) - pltpu.roll(bm, 1, 1),
            pltpu.roll(ah, LANES - 1, 1) - pltpu.roll(bh, 1, 1),
        )

    def ends(chunk):
        lane = lax.broadcasted_iota(jnp.int32, (chunk, LANES), 1)
        return lane == 0, lane == LANES - 1

    def ice_static(i):
        here = pl.ds(pl.multiple_of(EDGE - 8 + i * 8, 8), 8)
        for p in (0, 1):
            got = ice_coefficients(*(ice[f, p, here, :] for f in (STRENGTH, MASSX, COVER, U, V, WX, WY)))
            for f, x in enumerate(got):
                der[f, p, here, :] = x

    def ice_step():
        n = ICE_CHUNK
        first, last = ends(n)

        def stress(i):
            at = pl.multiple_of(EDGE - 8 + i * n, 8)
            here, north, south = pl.ds(at, n), pl.ds(at + 1, n), pl.ds(at - 1, n)
            exx = dx_pair(ice[U, 0, here, :], ice[U, 1, here, :], first, last)
            exv = dx_pair(ice[V, 0, here, :], ice[V, 1, here, :], first, last)
            for p in (0, 1):
                eyy = ice[V, p, north, :] - ice[V, p, south, :]
                shear = ice[U, p, north, :] - ice[U, p, south, :] + exv[p]
                got = stresses(
                    exx[p], eyy, shear, der[C1, p, here, :], der[C2, p, here, :], *(ice[f, p, here, :] for f in (S1, S2, S12))
                )
                for f, x in zip((S1, S2, S12), got):
                    ice[f, p, here, :] = x

        loop(full // n, stress)

        def velocity(i):
            at = pl.multiple_of(EDGE - 8 + i * n, 8)
            here, north, south = pl.ds(at, n), pl.ds(at + 1, n), pl.ds(at - 1, n)
            sums = [ice[S1, p, here, :] + ice[S2, p, here, :] for p in (0, 1)]
            dsum = dx_pair(sums[0], sums[1], first, last)
            dxy = dx_pair(ice[S12, 0, here, :], ice[S12, 1, here, :], first, last)
            f = cor[here, :]
            for p in (0, 1):
                fx = 0.25 * dsum[p] + 0.5 * (ice[S12, p, north, :] - ice[S12, p, south, :])
                dyy = (ice[S1, p, north, :] - ice[S2, p, north, :]) - (ice[S1, p, south, :] - ice[S2, p, south, :])
                fy = 0.5 * dxy[p] + 0.25 * dyy
                u, v = ice[U, p, here, :], ice[V, p, here, :]
                new_u, new_v = velocities(
                    fx,
                    fy,
                    u,
                    v,
                    der[RELAX, p, here, :],
                    der[INVM, p, here, :],
                    ice[COVER, p, here, :],
                    der[KU, p, here, :],
                    der[KV, p, here, :],
                    ice[OU, p, here, :],
                    ice[OV, p, here, :],
                    f,
                )
                ice[U, p, here, :] = new_u
                ice[V, p, here, :] = new_v

        loop(full // n, velocity)

    def ice_strip_static(w):
        for i in range(1, w + 2):
            fields = (STRENGTH, MASSX, COVER, U, V, WX, WY)
            got = ice_coefficients(*(ist[f, i] for f in fields))
            for f, x in enumerate(got):
                ider[f, i] = x

    def ice_strip_step(n):
        for i in range(1, n + 1):
            exx, exv = dx_strip(ist[U, i]), dx_strip(ist[V, i])
            eyy = ist[V, i - 1] - ist[V, i + 1]
            shear = ist[U, i - 1] - ist[U, i + 1] + exv
            got = stresses(exx, eyy, shear, ider[C1, i], ider[C2, i], *(ist[f, i] for f in (S1, S2, S12)))
            for f, x in zip((S1, S2, S12), got):
                ist[f, i] = x
        for i in range(2, n):
            fx = 0.25 * dx_strip(ist[S1, i] + ist[S2, i]) + 0.5 * (ist[S12, i - 1] - ist[S12, i + 1])
            dyy = (ist[S1, i - 1] - ist[S2, i - 1]) - (ist[S1, i + 1] - ist[S2, i + 1])
            fy = 0.5 * dx_strip(ist[S12, i]) + 0.25 * dyy
            new_u, new_v = velocities(
                fx,
                fy,
                ist[U, i],
                ist[V, i],
                ider[RELAX, i],
                ider[INVM, i],
                ist[COVER, i],
                ider[KU, i],
                ider[KV, i],
                ist[OU, i],
                ist[OV, i],
                row_coriolis(i),
            )
            ist[U, i] = new_u
            ist[V, i] = new_v

    def sea_coefficients(depth, land):
        return land / (1.0 + 0.1 / depth), 0.25 * depth

    def sea_static(i):
        here = pl.ds(pl.multiple_of(EDGE - 8 + i * 8, 8), 8)
        for p in (0, 1):
            a, b = sea_coefficients(sea[DEPTH, p, here, :], sea[LAND, p, here, :])
            der[0, p, here, :] = a
            der[1, p, here, :] = b

    def flows(tu, tv, part, slope, dlx, dly, f, sx, sy):
        east = part * (tu - slope * dlx + (0.5 * f) * tv + 0.5 * sx)
        north = part * (tv - slope * dly - (0.5 * f) * tu + 0.5 * sy)
        return east, north

    def sea_step():
        n = SEA_CHUNK
        first, last = ends(n)

        def level(i):
            at = pl.multiple_of(EDGE - 8 + i * n, 8)
            here, north, south = pl.ds(at, n), pl.ds(at + 1, n), pl.ds(at - 1, n)
            du = dx_pair(sea[TU, 0, here, :], sea[TU, 1, here, :], first, last)
            for p in (0, 1):
                dv = sea[TV, p, north, :] - sea[TV, p, south, :]
                sea[LEVEL, p, here, :] = sea[LAND, p, here, :] * (sea[LEVEL, p, here, :] - 0.25 * (du[p] + dv))

        loop(full // n, level)

        def flow(i):
            at = pl.multiple_of(EDGE - 8 + i * n, 8)
            here, north, south = pl.ds(at, n), pl.ds(at + 1, n), pl.ds(at - 1, n)
            dlx = dx_pair(sea[LEVEL, 0, here, :], sea[LEVEL, 1, here, :], first, last)
            f = cor[here, :]
            for p in (0, 1):
                dly = sea[LEVEL, p, north, :] - sea[LEVEL, p, south, :]
                east, nrth = flows(
                    sea[TU, p, here, :],
                    sea[TV, p, here, :],
                    der[0, p, here, :],
                    der[1, p, here, :],
                    dlx[p],
                    dly,
                    f,
                    sea[SX, p, here, :],
                    sea[SY, p, here, :],
                )
                sea[TU, p, here, :] = east
                sea[TV, p, here, :] = nrth

        loop(full // n, flow)

    def sea_strip_static(w):
        for i in range(2, w + 2):
            a, b = sea_coefficients(sst[DEPTH, i], sst[LAND, i])
            sder[0, i] = a
            sder[1, i] = b

    def sea_strip_step(n):
        for i in range(1, n + 1):
            dv = sst[TV, i - 1] - sst[TV, i + 1]
            sst[LEVEL, i] = sst[LAND, i] * (sst[LEVEL, i] - 0.25 * (dx_strip(sst[TU, i]) + dv))
        for i in range(2, n):
            dly = sst[LEVEL, i - 1] - sst[LEVEL, i + 1]
            east, nrth = flows(
                sst[TU, i],
                sst[TV, i],
                sder[0, i],
                sder[1, i],
                dx_strip(sst[LEVEL, i]),
                dly,
                row_coriolis(i),
                sst[SX, i],
                sst[SY, i],
            )
            sst[TU, i] = east
            sst[TV, i] = nrth

    stage(ice_ex[0], ice)
    greeted = 2 + 3 * (gy < bands - 1).astype(jnp.int32) + 3 * (gy > 0).astype(jnp.int32)
    pl.semaphore_wait(barrier, greeted + (blocks - 1) * is_top.astype(jnp.int32))
    start(ice_ex[0])
    stage(sea_ex, sea)
    start(sea_ex)

    state = (U, V, S1, S2, S12)
    for number, ex in enumerate(ice_ex):
        if number:
            stage(ex, ice)
            start(ex)
        wait_recv(ex)
        unpack(ex, ice, MASSX)
        wait_strips(ex)

        @pl.when(is_top)
        def _(ex=ex, number=number):
            strip_load(ex, ist)
            fold(ist, ice, state + ((STRENGTH, MASSX, COVER, WX, WY) if number == 0 else ()), ICE_SIGNS)
            if number == 0:
                ice_strip_static(ex.width)

        if number == 0:
            loop(full // 8, ice_static)
        for step in range(ex.steps):
            if step:

                @pl.when(is_top)
                def _(n=ex.width - 2 * (step - 1)):
                    ice_strip_step(n)
                    fold(ist, ice, state, ICE_SIGNS)

            ice_step()

    outs = [
        pltpu.make_async_copy(ice.at[U : V + 1, 0, own], vel_out, out_sem.at[0]),
        pltpu.make_async_copy(ice.at[S1 : S12 + 1, 0, own], str_out, out_sem.at[1]),
    ]

    def surface(i):
        here = pl.ds(pl.multiple_of(EDGE + i * 8, 8), 8)
        cover = ice[COVER, 0, here, :]
        rx, ry = ice[U, 0, here, :] - ice[OU, 0, here, :], ice[V, 0, here, :] - ice[OV, 0, here, :]
        drag = cover * (0.5 * jnp.sqrt(rx * rx + ry * ry))
        sea[SX, 0, here, :] = drag * rx + (1.0 - cover) * ice[WX, 0, here, :]
        sea[SY, 0, here, :] = drag * ry + (1.0 - cover) * ice[WY, 0, here, :]

    loop(rows // 8, surface)
    stage(surf_ex, sea)
    start(surf_ex)
    for copy in outs:
        copy.start()
    flow_state = (LEVEL, TU, TV)
    for number, ex in enumerate([sea_ex] + later_ex):
        if number:
            stage(ex, sea)
            start(ex)
        wait_recv(ex)
        unpack(ex, sea, DEPTH)
        wait_strips(ex)

        @pl.when(is_top)
        def _(ex=ex, number=number):
            strip_load(ex, sst)
            fold(sst, sea, flow_state + ((DEPTH, LAND) if number == 0 else ()), SEA_SIGNS)
            if number == 0:
                sea_strip_static(ex.width)

        if number == 0:
            loop(full // 8, sea_static)
            wait_recv(surf_ex)
            unpack(surf_ex, sea, DEPTH)
            wait_strips(surf_ex)

            @pl.when(is_top)
            def _():
                strip_load(surf_ex, sst)

        for step in range(ex.steps):
            if step:

                @pl.when(is_top)
                def _(n=ex.width - 2 * (step - 1)):
                    sea_strip_step(n)
                    fold(sst, sea, flow_state, SEA_SIGNS)

            sea_step()

    outs += [
        pltpu.make_async_copy(sea.at[LEVEL, 0, own], level_out, out_sem.at[2]),
        pltpu.make_async_copy(sea.at[TU : TV + 1, 0, own], trans_out, out_sem.at[3]),
    ]
    for copy in outs[2:]:
        copy.start()
    for ex in ice_ex + [sea_ex, surf_ex] + later_ex:
        wait_send(ex)
    for copy in outs:
        copy.wait()


def per_device(blocks, bands, *args):
    f32 = jnp.float32
    rows = args[2].shape[0]
    tall = rows + 2 * EDGE
    ice_ex, sea_ex, surf_ex, later_ex = plan(rows)
    depth = 2 + 2 * max(ICE_GROUPS + SEA_GROUPS)
    scratch = dict(
        ice=pltpu.VMEM((12, 2, tall, LANES), f32),
        der=pltpu.VMEM((6, 2, tall, LANES), f32),
        sea=pltpu.VMEM((7, 2, tall, LANES), f32),
        cor=pltpu.VMEM((tall, LANES), f32),
        ist=pltpu.VMEM((12, depth, blocks, LANES), f32),
        ider=pltpu.VMEM((6, depth, blocks, LANES), f32),
        sst=pltpu.VMEM((7, depth, blocks, LANES), f32),
        sder=pltpu.VMEM((2, depth, blocks, LANES), f32),
        masks=pltpu.VMEM((2, rows, LANES), jnp.int32),
        partner=pltpu.VMEM((1, LANES), jnp.int32),
        perm=pltpu.VMEM((blocks, LANES), jnp.int32),
        in_sem=pltpu.SemaphoreType.DMA((11,)),
        out_sem=pltpu.SemaphoreType.DMA((4,)),
    )
    for ex in ice_ex + [sea_ex, surf_ex] + later_ex:
        for part, space in ex.scratch(blocks).items():
            scratch[ex.name, part] = space

    def body(*refs):
        kernel_body(blocks, bands, list(scratch), *refs)

    sds = jax.ShapeDtypeStruct
    args = args[:-1] + (args[-1].reshape(1, LANES),)
    anywhere = pl.BlockSpec(memory_space=pl.ANY)
    return pl.pallas_call(
        body,
        out_shape=(
            sds((2, rows, LANES), f32),
            sds((3, rows, LANES), f32),
            sds((rows, LANES), f32),
            sds((2, rows, LANES), f32),
        ),
        in_specs=[anywhere] * 11,
        out_specs=(anywhere,) * 4,
        scratch_shapes=list(scratch.values()),
        compiler_params=pltpu.CompilerParams(
            collective_id=0, has_side_effects=True, vmem_limit_bytes=67043328
        ),
        name="coupled_step",
    )(*args)


def solution(mesh):
    blocks, bands = mesh.shape["gx"], mesh.shape["gy"]
    flat, stacked = P("gy", "gx"), P(None, "gy", "gx")
    in_specs = (stacked, stacked, flat, flat, stacked, flat, stacked, flat, flat, flat, P("gx"))

    def step(*args):
        return per_device(blocks, bands, *args)

    return jax.shard_map(
        step, mesh=mesh, in_specs=in_specs, out_specs=(stacked, stacked, flat, stacked), check_vma=False
    )
```

time: 592 us -> 67.2 us (0.11)
  the two profiles are of different devices: /device:TPU:8 before, /device:TPU:25 now
where the time goes in v1:
time: 67.2 us; the launch traced here: 67.1 us
  Pallas kernels  62.1 us (92%)
  local copies, waits for them, and re-layouts  4.35 us (6%)
    pallas_call x1, Pallas kernels, per_device(): pl.pallas_call(body, out_shape=(sds((2, rows, LANES), f32), sds((3, rows,...  62.1 us
    unnamed x10, local copies, waits for them, and re-layouts  4.35 us

profile of v1, /device:TPU:25, one launch (start us, length us, event | category | flops | bytes accessed | tf_op | source)
XLA Modules:
  0.0 67.1 jit_solution(2268364197338875228)
XLA Ops:
  0.6 62.1 %coupled_step.1 = (f32[2,224,128]{2,1,0:T(8,128)}, f32[3,224,128]{2,1,0:T(8,128)}, f32[224,128]{1,0:T(8,128)}, f32[2,224,128]{2,1,0:T(8,128)}) custom-call(f32[2,224,128]{2,1,0:T(8,128)} %refs_0_.1, f32[3,224,128]{2,1,0:T(8,128)} %refs_1_.1, f32[224,128]{1,0:T(8,128)} %refs_2_.1, f32[224,128]{1,0:T(8,128)} %refs_3_.1, f32[2,224,128]{2,1,0:T(8,128)} %refs_4_.1, ...), custom_call_target="tpu_custom_call" | custom-call | tf_op jit(solution)/shard_map/coupled_step/pallas_call | solution.py:735
  62.7 0.0 copy-start
  62.7 1.7 %copy.19 = f32[2,224,128]{2,1,0:T(8,128)} copy(f32[2,224,128]{2,1,0:T(8,128)} %get-tuple-element.8) | data formatting | bytes 458752
  64.4 0.0 copy-done
  64.4 0.0 copy-start.2
  64.4 0.7 %copy.20 = f32[3,224,128]{2,1,0:T(8,128)} copy(f32[3,224,128]{2,1,0:T(8,128)S(1)} %copy-done) | data formatting | bytes 688128
  65.1 0.3 copy-done.2
  65.4 0.0 copy-start.1
  65.4 0.6 copy.21
  66.0 0.3 copy-done.1
  66.4 0.7 %copy.22 = f32[2,224,128]{2,1,0:T(8,128)} copy(f32[2,224,128]{2,1,0:T(8,128)S(1)} %copy-done.1) | data formatting | bytes 458752
Async XLA Ops:
  62.7 1.7 %copy-start = (f32[3,224,128]{2,1,0:T(8,128)S(1)}, f32[3,224,128]{2,1,0:T(8,128)}, u32[]{:S(2)}) copy-start(f32[3,224,128]{2,1,0:T(8,128)} %get-tuple-element.9) | copy-start | bytes 1032196
  64.4 1.0 %copy-start.2 = (f32[224,128]{1,0:T(8,128)S(1)}, f32[224,128]{1,0:T(8,128)}, u32[]{:S(2)}) copy-start(f32[224,128]{1,0:T(8,128)} %get-tuple-element.10) | copy-start | bytes 344068
  65.4 1.0 %copy-start.1 = (f32[2,224,128]{2,1,0:T(8,128)S(1)}, f32[2,224,128]{2,1,0:T(8,128)}, u32[]{:S(2)}) copy-start(f32[2,224,128]{2,1,0:T(8,128)} %get-tuple-element.11) | copy-start | bytes 688132

commit v2 on v1

--- a/solution.py
+++ b/solution.py
@@ -10,8 +10,8 @@
 ICE_GROUPS = (2, 2)
 SEA_GROUPS = (3, 3)
 EDGE = 16
-ICE_CHUNK = 24
-SEA_CHUNK = 24
+ICE_CHUNK = 240
+SEA_CHUNK = 240
 LANES = 128
 MESH_ID = pl.DeviceIdType.MESH
 
@@ -142,14 +142,11 @@
         copy.start()
 
     def loop(count, body):
-        def one(i, carry):
+        for i in range(count):
             body(i)
-            return carry
-
-        lax.fori_loop(0, count, one, 0)
 
     def coriolis(i):
-        at = pl.multiple_of(i * 8, 8)
+        at = i * 8
         r = lax.broadcasted_iota(jnp.int32, (8, LANES), 0) + (gy * rows + at - EDGE)
         angle = jnp.pi * ((r.astype(jnp.float32) + 0.5) / total_rows - 0.5)
         cor[pl.ds(at, 8), :] = 0.5 * jnp.sin(angle)
@@ -159,7 +156,7 @@
         copy.wait()
 
     def prepare(i):
-        at = pl.multiple_of(i * 8, 8)
+        at = i * 8
         here, m = pl.ds(at + EDGE, 8), pl.ds(at, 8)
         land = masks[0, m, :].astype(jnp.float32)
         cover = land * masks[1, m, :].astype(jnp.float32)
@@ -190,7 +187,7 @@
             for g in range(ex.groups):
                 for k, f in enumerate(ex.fields):
                     at = g * ex.group_lanes + k * w
-                    here = pl.ds(pl.multiple_of(EDGE + g * ex.group_rows + i * 8, 8), 8)
+                    here = pl.ds(EDGE + g * ex.group_rows + i * 8, 8)
                     x = store[f, 0, here, :]
                     a = pltpu.roll(x, at, 1) if at else x
                     b = pltpu.roll(x, (at + w) % LANES, 1) if (at + w) % LANES else x
@@ -200,7 +197,7 @@
                         keep = lane8 < at
                         to_west = jnp.where(keep, to_west, a)
                         to_east = jnp.where(keep, to_east, b)
-            m = pl.ds(pl.multiple_of(i * 8, 8), 8)
+            m = pl.ds(i * 8, 8)
             ref[ex.name, "west"][m, :] = to_west
             ref[ex.name, "east"][m, :] = to_east
 
@@ -330,9 +327,9 @@
                 store[f, 1, target, :] = jnp.where(lane8 < LANES // 2, a, b)
 
         def main(i):
-            source = pl.ds(pl.multiple_of(i * 8, 8), 8)
+            source = pl.ds(i * 8, 8)
             for g in range(ex.groups):
-                place(source, g, pl.ds(pl.multiple_of(EDGE + g * n + i * 8, 8), 8))
+                place(source, g, pl.ds(EDGE + g * n + i * 8, 8))
 
         loop(n // 8, main)
 
@@ -429,7 +426,7 @@
         return lane == 0, lane == LANES - 1
 
     def ice_static(i):
-        here = pl.ds(pl.multiple_of(EDGE - 8 + i * 8, 8), 8)
+        here = pl.ds(EDGE - 8 + i * 8, 8)
         for p in (0, 1):
             got = ice_coefficients(*(ice[f, p, here, :] for f in (STRENGTH, MASSX, COVER, U, V, WX, WY)))
             for f, x in enumerate(got):
@@ -440,7 +437,7 @@
         first, last = ends(n)
 
         def stress(i):
-            at = pl.multiple_of(EDGE - 8 + i * n, 8)
+            at = EDGE - 8 + i * n
             here, north, south = pl.ds(at, n), pl.ds(at + 1, n), pl.ds(at - 1, n)
             exx = dx_pair(ice[U, 0, here, :], ice[U, 1, here, :], first, last)
             exv = dx_pair(ice[V, 0, here, :], ice[V, 1, here, :], first, last)
@@ -456,7 +453,7 @@
         loop(full // n, stress)
 
         def velocity(i):
-            at = pl.multiple_of(EDGE - 8 + i * n, 8)
+            at = EDGE - 8 + i * n
             here, north, south = pl.ds(at, n), pl.ds(at + 1, n), pl.ds(at - 1, n)
             sums = [ice[S1, p, here, :] + ice[S2, p, here, :] for p in (0, 1)]
             dsum = dx_pair(sums[0], sums[1], first, last)
@@ -526,7 +523,7 @@
         return land / (1.0 + 0.1 / depth), 0.25 * depth
 
     def sea_static(i):
-        here = pl.ds(pl.multiple_of(EDGE - 8 + i * 8, 8), 8)
+        here = pl.ds(EDGE - 8 + i * 8, 8)
         for p in (0, 1):
             a, b = sea_coefficients(sea[DEPTH, p, here, :], sea[LAND, p, here, :])
             der[0, p, here, :] = a
@@ -542,7 +539,7 @@
         first, last = ends(n)
 
         def level(i):
-            at = pl.multiple_of(EDGE - 8 + i * n, 8)
+            at = EDGE - 8 + i * n
             here, north, south = pl.ds(at, n), pl.ds(at + 1, n), pl.ds(at - 1, n)
             du = dx_pair(sea[TU, 0, here, :], sea[TU, 1, here, :], first, last)
             for p in (0, 1):
@@ -552,7 +549,7 @@
         loop(full // n, level)
 
         def flow(i):
-            at = pl.multiple_of(EDGE - 8 + i * n, 8)
+            at = EDGE - 8 + i * n
             here, north, south = pl.ds(at, n), pl.ds(at + 1, n), pl.ds(at - 1, n)
             dlx = dx_pair(sea[LEVEL, 0, here, :], sea[LEVEL, 1, here, :], first, last)
             f = cor[here, :]
@@ -635,13 +632,8 @@
 
             ice_step()
 
-    outs = [
-        pltpu.make_async_copy(ice.at[U : V + 1, 0, own], vel_out, out_sem.at[0]),
-        pltpu.make_async_copy(ice.at[S1 : S12 + 1, 0, own], str_out, out_sem.at[1]),
-    ]
-
     def surface(i):
-        here = pl.ds(pl.multiple_of(EDGE + i * 8, 8), 8)
+        here = pl.ds(EDGE + i * 8, 8)
         cover = ice[COVER, 0, here, :]
         rx, ry = ice[U, 0, here, :] - ice[OU, 0, here, :], ice[V, 0, here, :] - ice[OV, 0, here, :]
         drag = cover * (0.5 * jnp.sqrt(rx * rx + ry * ry))
@@ -651,7 +643,13 @@
     loop(rows // 8, surface)
     stage(surf_ex, sea)
     start(surf_ex)
-    for copy in outs:
+    outs = [
+        pltpu.make_async_copy(ice.at[U : V + 1, 0, own], vel_out, out_sem.at[0]),
+        pltpu.make_async_copy(ice.at[S1 : S12 + 1, 0, own], str_out, out_sem.at[1]),
+        pltpu.make_async_copy(sea.at[LEVEL, 0, own], level_out, out_sem.at[2]),
+        pltpu.make_async_copy(sea.at[TU : TV + 1, 0, own], trans_out, out_sem.at[3]),
+    ]
+    for copy in outs[:2]:
         copy.start()
     flow_state = (LEVEL, TU, TV)
     for number, ex in enumerate([sea_ex] + later_ex):
@@ -689,15 +687,25 @@
 
             sea_step()
 
-    outs += [
-        pltpu.make_async_copy(sea.at[LEVEL, 0, own], level_out, out_sem.at[2]),
-        pltpu.make_async_copy(sea.at[TU : TV + 1, 0, own], trans_out, out_sem.at[3]),
-    ]
     for copy in outs[2:]:
         copy.start()
     for ex in ice_ex + [sea_ex, surf_ex] + later_ex:
         wait_send(ex)
     for copy in outs:
+        copy.wait()
+
+
+def write_out(*refs):
+    sources, targets, held, sems = refs[:4], refs[4:8], refs[8:12], refs[12]
+    pairs = list(zip(sources, held, targets))
+    reads = [pltpu.make_async_copy(a, b, sems.at[0, i]) for i, (a, b, _) in enumerate(pairs)]
+    writes = [pltpu.make_async_copy(b, c, sems.at[1, i]) for i, (_, b, c) in enumerate(pairs)]
+    for copy in reads:
+        copy.start()
+    for read, write in zip(reads, writes):
+        read.wait()
+        write.start()
+    for copy in writes:
         copy.wait()
 
 
@@ -731,23 +739,33 @@
 
     sds = jax.ShapeDtypeStruct
     args = args[:-1] + (args[-1].reshape(1, LANES),)
-    anywhere = pl.BlockSpec(memory_space=pl.ANY)
-    return pl.pallas_call(
+    shapes = (
+        sds((2, rows, LANES), f32),
+        sds((3, rows, LANES), f32),
+        sds((rows, LANES), f32),
+        sds((2, rows, LANES), f32),
+    )
+    far = pl.BlockSpec(memory_space=pltpu.HBM)
+    results = pl.pallas_call(
         body,
-        out_shape=(
-            sds((2, rows, LANES), f32),
-            sds((3, rows, LANES), f32),
-            sds((rows, LANES), f32),
-            sds((2, rows, LANES), f32),
-        ),
-        in_specs=[anywhere] * 11,
-        out_specs=(anywhere,) * 4,
+        out_shape=shapes,
+        in_specs=[far] * 11,
+        out_specs=(far,) * 4,
         scratch_shapes=list(scratch.values()),
         compiler_params=pltpu.CompilerParams(
             collective_id=0, has_side_effects=True, vmem_limit_bytes=67043328
         ),
         name="coupled_step",
     )(*args)
+    return pl.pallas_call(
+        write_out,
+        out_shape=shapes,
+        in_specs=[far] * 4,
+        out_specs=(far,) * 4,
+        scratch_shapes=[pltpu.VMEM(x.shape, f32) for x in shapes] + [pltpu.SemaphoreType.DMA((2, 4))],
+        compiler_params=pltpu.CompilerParams(vmem_limit_bytes=67043328),
+        name="write_out",
+    )(*results)
 
 
 def solution(mesh):

time: 67.2 us -> 46.7 us (0.69)
  Pallas kernels: 62.1 us -> 45.9 us
  local copies, waits for them, and re-layouts: 4.35 us -> 0 us
    pallas_call x1 -> x2, Pallas kernels: 62.1 us -> 45.9 us  [the longest x1 43.9 us: per_device(): pl.pallas_call(body, out_shape=shapes, in_specs=[far] * 11, out_specs=(fa...]
    unnamed x10 -> x0, local copies, waits for them, and re-layouts: 4.35 us -> none
where the time goes in v2:
time: 46.7 us; the launch traced here: 46.6 us
  Pallas kernels  45.9 us (98%)
  between operations  0.64 us (1%)
    pallas_call x1, Pallas kernels, per_device(): pl.pallas_call(body, out_shape=shapes, in_specs=[far] * 11, out_specs=(fa...  43.9 us
    pallas_call x1, Pallas kernels, per_device(): pl.pallas_call(write_out, out_shape=shapes, in_specs=[far] * 4, out_specs...  2.01 us

profile of v2, /device:TPU:25, one launch (start us, length us, event | category | flops | bytes accessed | tf_op | source)
XLA Modules:
  0.0 46.6 jit_solution(16828206048786685105)
XLA Ops:
  0.6 43.9 %coupled_step.1 = (f32[2,224,128]{2,1,0:T(8,128)}, f32[3,224,128]{2,1,0:T(8,128)}, f32[224,128]{1,0:T(8,128)}, f32[2,224,128]{2,1,0:T(8,128)}) custom-call(f32[2,224,128]{2,1,0:T(8,128)} %refs_0_.1, f32[3,224,128]{2,1,0:T(8,128)} %refs_1_.1, f32[224,128]{1,0:T(8,128)} %refs_2_.1, f32[224,128]{1,0:T(8,128)} %refs_3_.1, f32[2,224,128]{2,1,0:T(8,128)} %refs_4_.1, ...), custom_call_target="tpu_custom_call" | custom-call | tf_op jit(solution)/shard_map/coupled_step/pallas_call | solution.py:749
  44.6 2.0 %write_out.1 = (f32[2,224,128]{2,1,0:T(8,128)}, f32[3,224,128]{2,1,0:T(8,128)}, f32[224,128]{1,0:T(8,128)}, f32[2,224,128]{2,1,0:T(8,128)}) custom-call(f32[2,224,128]{2,1,0:T(8,128)} %get-tuple-element.8.refs_0_, f32[3,224,128]{2,1,0:T(8,128)} %get-tuple-element.9.refs_1_, f32[224,128]{1,0:T(8,128)} %get-tuple-element.10.refs_2_, ...), custom_call_target="tpu_custom_call" | custom-call | tf_op jit(solution)/shard_map/write_out/pallas_call | solution.py:760

commit v3 on v2

--- a/solution.py
+++ b/solution.py
@@ -7,11 +7,11 @@
 from jax.experimental.pallas import tpu as pltpu
 from jax.sharding import PartitionSpec as P
 
-ICE_GROUPS = (2, 2)
+ICE_GROUPS = (4,)
 SEA_GROUPS = (3, 3)
 EDGE = 16
-ICE_CHUNK = 240
-SEA_CHUNK = 240
+ICE_CHUNK = 24
+SEA_CHUNK = 24
 LANES = 128
 MESH_ID = pl.DeviceIdType.MESH
 
@@ -26,7 +26,8 @@
     def __init__(self, name, fields, steps, rows):
         self.name, self.fields, self.steps = name, fields, steps
         self.width = 2 * steps
-        self.groups = 4 if len(fields) * self.width <= 32 else 2
+        lanes = len(fields) * self.width
+        self.groups = 4 if lanes <= 32 else 2 if lanes <= 64 else 1
         self.group_lanes = LANES // self.groups
         assert len(fields) * self.width <= self.group_lanes
         self.group_rows = rows // self.groups
@@ -432,8 +433,13 @@
             for f, x in enumerate(got):
                 der[f, p, here, :] = x
 
-    def ice_step():
+    def dx_own(m, h, first, last):
+        am, bm = jnp.where(first, h, m), jnp.where(last, h, m)
+        return (pltpu.roll(am, LANES - 1, 1) - pltpu.roll(bm, 1, 1),)
+
+    def ice_step(final):
         n = ICE_CHUNK
+        planes, dx = ((0,), dx_own) if final else ((0, 1), dx_pair)
         first, last = ends(n)
 
         def stress(i):
@@ -456,10 +462,10 @@
             at = EDGE - 8 + i * n
             here, north, south = pl.ds(at, n), pl.ds(at + 1, n), pl.ds(at - 1, n)
             sums = [ice[S1, p, here, :] + ice[S2, p, here, :] for p in (0, 1)]
-            dsum = dx_pair(sums[0], sums[1], first, last)
-            dxy = dx_pair(ice[S12, 0, here, :], ice[S12, 1, here, :], first, last)
+            dsum = dx(sums[0], sums[1], first, last)
+            dxy = dx(ice[S12, 0, here, :], ice[S12, 1, here, :], first, last)
             f = cor[here, :]
-            for p in (0, 1):
+            for p in planes:
                 fx = 0.25 * dsum[p] + 0.5 * (ice[S12, p, north, :] - ice[S12, p, south, :])
                 dyy = (ice[S1, p, north, :] - ice[S2, p, north, :]) - (ice[S1, p, south, :] - ice[S2, p, south, :])
                 fy = 0.5 * dxy[p] + 0.25 * dyy
@@ -534,8 +540,9 @@
         north = part * (tv - slope * dly - (0.5 * f) * tu + 0.5 * sy)
         return east, north
 
-    def sea_step():
+    def sea_step(final):
         n = SEA_CHUNK
+        planes, dx = ((0,), dx_own) if final else ((0, 1), dx_pair)
         first, last = ends(n)
 
         def level(i):
@@ -551,9 +558,9 @@
         def flow(i):
             at = EDGE - 8 + i * n
             here, north, south = pl.ds(at, n), pl.ds(at + 1, n), pl.ds(at - 1, n)
-            dlx = dx_pair(sea[LEVEL, 0, here, :], sea[LEVEL, 1, here, :], first, last)
+            dlx = dx(sea[LEVEL, 0, here, :], sea[LEVEL, 1, here, :], first, last)
             f = cor[here, :]
-            for p in (0, 1):
+            for p in planes:
                 dly = sea[LEVEL, p, north, :] - sea[LEVEL, p, south, :]
                 east, nrth = flows(
                     sea[TU, p, here, :],
@@ -630,7 +637,7 @@
                     ice_strip_step(n)
                     fold(ist, ice, state, ICE_SIGNS)
 
-            ice_step()
+            ice_step(step == ex.steps - 1)
 
     def surface(i):
         here = pl.ds(EDGE + i * 8, 8)
@@ -685,7 +692,7 @@
                     sea_strip_step(n)
                     fold(sst, sea, flow_state, SEA_SIGNS)
 
-            sea_step()
+            sea_step(step == ex.steps - 1)
 
     for copy in outs[2:]:
         copy.start()

time: 46.7 us -> 44.7 us (0.957)
  Pallas kernels: 45.9 us -> 43.9 us
    pallas_call x1, Pallas kernels: 43.9 us -> 41.9 us  [per_device(): pl.pallas_call(body, out_shape=shapes, in_specs=[far] * 11, out_specs=(fa...]
where the time goes in v3:
time: 44.7 us; the launch traced here: 44.6 us
  Pallas kernels  43.9 us (98%)
  between operations  0.64 us (1%)
    pallas_call x1, Pallas kernels, per_device(): pl.pallas_call(body, out_shape=shapes, in_specs=[far] * 11, out_specs=(fa...  41.9 us
    pallas_call x1, Pallas kernels, per_device(): pl.pallas_call(write_out, out_shape=shapes, in_specs=[far] * 4, out_specs...  2.01 us

profile of v3, /device:TPU:25, one launch (start us, length us, event | category | flops | bytes accessed | tf_op | source)
XLA Modules:
  0.0 44.6 jit_solution(18255051804763544164)
XLA Ops:
  0.6 41.9 %coupled_step.1 = (f32[2,224,128]{2,1,0:T(8,128)}, f32[3,224,128]{2,1,0:T(8,128)}, f32[224,128]{1,0:T(8,128)}, f32[2,224,128]{2,1,0:T(8,128)}) custom-call(f32[2,224,128]{2,1,0:T(8,128)} %refs_0_.1, f32[3,224,128]{2,1,0:T(8,128)} %refs_1_.1, f32[224,128]{1,0:T(8,128)} %refs_2_.1, f32[224,128]{1,0:T(8,128)} %refs_3_.1, f32[2,224,128]{2,1,0:T(8,128)} %refs_4_.1, ...), custom_call_target="tpu_custom_call" | custom-call | tf_op jit(solution)/shard_map/coupled_step/pallas_call | solution.py:756
  42.6 2.0 %write_out.1 = (f32[2,224,128]{2,1,0:T(8,128)}, f32[3,224,128]{2,1,0:T(8,128)}, f32[224,128]{1,0:T(8,128)}, f32[2,224,128]{2,1,0:T(8,128)}) custom-call(f32[2,224,128]{2,1,0:T(8,128)} %get-tuple-element.8.refs_0_, f32[3,224,128]{2,1,0:T(8,128)} %get-tuple-element.9.refs_1_, f32[224,128]{1,0:T(8,128)} %get-tuple-element.10.refs_2_, ...), custom_call_target="tpu_custom_call" | custom-call | tf_op jit(solution)/shard_map/write_out/pallas_call | solution.py:767

commit v4 on v3

--- a/solution.py
+++ b/solution.py
@@ -609,7 +609,6 @@
     pl.semaphore_wait(barrier, greeted + (blocks - 1) * is_top.astype(jnp.int32))
     start(ice_ex[0])
     stage(sea_ex, sea)
-    start(sea_ex)
 
     state = (U, V, S1, S2, S12)
     for number, ex in enumerate(ice_ex):
@@ -619,6 +618,8 @@
         wait_recv(ex)
         unpack(ex, ice, MASSX)
         wait_strips(ex)
+        if number == 0:
+            start(sea_ex)
 
         @pl.when(is_top)
         def _(ex=ex, number=number):
@@ -659,10 +660,14 @@
     for copy in outs[:2]:
         copy.start()
     flow_state = (LEVEL, TU, TV)
+    unsent = ice_ex + [sea_ex, surf_ex]
     for number, ex in enumerate([sea_ex] + later_ex):
         if number:
             stage(ex, sea)
             start(ex)
+            while unsent:
+                wait_send(unsent.pop())
+            unsent.append(ex)
         wait_recv(ex)
         unpack(ex, sea, DEPTH)
         wait_strips(ex)
@@ -696,7 +701,7 @@
 
     for copy in outs[2:]:
         copy.start()
-    for ex in ice_ex + [sea_ex, surf_ex] + later_ex:
+    for ex in unsent:
         wait_send(ex)
     for copy in outs:
         copy.wait()

time: 44.7 us -> 44.3 us (level)
  no operation moved by 1% of the time
where the time goes in v4:
time: 44.3 us; the launch traced here: 44.2 us
  Pallas kernels  43.6 us (98%)
  between operations  0.64 us (1%)
    pallas_call x1, Pallas kernels, per_device(): pl.pallas_call(body, out_shape=shapes, in_specs=[far] * 11, out_specs=(fa...  41.6 us
    pallas_call x1, Pallas kernels, per_device(): pl.pallas_call(write_out, out_shape=shapes, in_specs=[far] * 4, out_specs...  2.01 us

profile of v4, /device:TPU:25, one launch (start us, length us, event | category | flops | bytes accessed | tf_op | source)
XLA Modules:
  0.0 44.2 jit_solution(14012647874697617249)
XLA Ops:
  0.6 41.6 %coupled_step.1 = (f32[2,224,128]{2,1,0:T(8,128)}, f32[3,224,128]{2,1,0:T(8,128)}, f32[224,128]{1,0:T(8,128)}, f32[2,224,128]{2,1,0:T(8,128)}) custom-call(f32[2,224,128]{2,1,0:T(8,128)} %refs_0_.1, f32[3,224,128]{2,1,0:T(8,128)} %refs_1_.1, f32[224,128]{1,0:T(8,128)} %refs_2_.1, f32[224,128]{1,0:T(8,128)} %refs_3_.1, f32[2,224,128]{2,1,0:T(8,128)} %refs_4_.1, ...), custom_call_target="tpu_custom_call" | custom-call | tf_op jit(solution)/shard_map/coupled_step/pallas_call | solution.py:761
  42.2 2.0 %write_out.1 = (f32[2,224,128]{2,1,0:T(8,128)}, f32[3,224,128]{2,1,0:T(8,128)}, f32[224,128]{1,0:T(8,128)}, f32[2,224,128]{2,1,0:T(8,128)}) custom-call(f32[2,224,128]{2,1,0:T(8,128)} %get-tuple-element.8.refs_0_, f32[3,224,128]{2,1,0:T(8,128)} %get-tuple-element.9.refs_1_, f32[224,128]{1,0:T(8,128)} %get-tuple-element.10.refs_2_, ...), custom_call_target="tpu_custom_call" | custom-call | tf_op jit(solution)/shard_map/write_out/pallas_call | solution.py:772

commit v5 on v4

--- a/solution.py
+++ b/solution.py
@@ -249,18 +249,13 @@
 
         @pl.when(is_top)
         def _():
-            def one(j, carry):
+            for j in range(1, blocks):
                 x = lax.rem(gx + j, blocks)
-                gap = lax.rem(x + gx + 1, blocks)
-                near = (j <= reach) | (j >= blocks - reach) | (gap <= reach) | (gap >= blocks - reach)
-
-                @pl.when(near)
-                def _():
+                if j <= reach or j >= blocks - reach:
                     action(x)
-
-                return carry
-
-            lax.fori_loop(1, blocks, one, 0)
+                else:
+                    gap = lax.rem(x + gx + 1, blocks)
+                    pl.when((gap <= reach) | (gap >= blocks - reach))(lambda x=x: action(x))
 
     def start(ex):
         each_strip(ex, lambda x: strip_copy(ex, x, gx).start())

time: 44.3 us -> 43.9 us (level)
  no operation moved by 1% of the time
where the time goes in v5:
time: 43.9 us; the launch traced here: 43.8 us
  Pallas kernels  43.2 us (98%)
  between operations  0.64 us (1%)
    pallas_call x1, Pallas kernels, per_device(): pl.pallas_call(body, out_shape=shapes, in_specs=[far] * 11, out_specs=(fa...  41.2 us
    pallas_call x1, Pallas kernels, per_device(): pl.pallas_call(write_out, out_shape=shapes, in_specs=[far] * 4, out_specs...  2.01 us

profile of v5, /device:TPU:25, one launch (start us, length us, event | category | flops | bytes accessed | tf_op | source)
XLA Modules:
  0.0 43.8 jit_solution(1297899676023519758)
XLA Ops:
  0.6 41.2 %coupled_step.1 = (f32[2,224,128]{2,1,0:T(8,128)}, f32[3,224,128]{2,1,0:T(8,128)}, f32[224,128]{1,0:T(8,128)}, f32[2,224,128]{2,1,0:T(8,128)}) custom-call(f32[2,224,128]{2,1,0:T(8,128)} %refs_0_.1, f32[3,224,128]{2,1,0:T(8,128)} %refs_1_.1, f32[224,128]{1,0:T(8,128)} %refs_2_.1, f32[224,128]{1,0:T(8,128)} %refs_3_.1, f32[2,224,128]{2,1,0:T(8,128)} %refs_4_.1, ...), custom_call_target="tpu_custom_call" | custom-call | tf_op jit(solution)/shard_map/coupled_step/pallas_call | solution.py:756
  41.8 2.0 %write_out.1 = (f32[2,224,128]{2,1,0:T(8,128)}, f32[3,224,128]{2,1,0:T(8,128)}, f32[224,128]{1,0:T(8,128)}, f32[2,224,128]{2,1,0:T(8,128)}) custom-call(f32[2,224,128]{2,1,0:T(8,128)} %get-tuple-element.8.refs_0_, f32[3,224,128]{2,1,0:T(8,128)} %get-tuple-element.9.refs_1_, f32[224,128]{1,0:T(8,128)} %get-tuple-element.10.refs_2_, ...), custom_call_target="tpu_custom_call" | custom-call | tf_op jit(solution)/shard_map/write_out/pallas_call | solution.py:767
